TPU v7x, 32 devices: a whole 2x2x4 slice. The times are simulated.
32 devices in a mesh: rep: 2 (over x), dp: 16 (over y, z, core).
Axes of the slice: x: 2, y: 2, z: 4, core: 2. Of those that a mesh axis runs over, the one named last changes fastest.
Arguments:
- x: bfloat16 [32, 2048, 640], P(('rep', 'dp')), parts along dimension 0
- dy: bfloat16 [32, 2048, 640], P(('rep', 'dp')), parts along dimension 0
- w_gate: bfloat16 [2, 640, 2560], replicated
- w_up: bfloat16 [2, 640, 2560], replicated
- w_down: bfloat16 [2, 2560, 640], replicated
- m_w_gate: float32 [2, 640, 2560], P(None, 'dp')
- m_w_up: float32 [2, 640, 2560], P(None, 'dp')
- m_w_down: float32 [2, 2560, 640], P(None, 'dp')
- v_w_gate: float32 [2, 640, 2560], P(None, 'dp')
- v_w_up: float32 [2, 640, 2560], P(None, 'dp')
- v_w_down: float32 [2, 2560, 640], P(None, 'dp')
Outputs:
- output 1: bfloat16 [4, 640, 2560], P('rep'), parts along dimension 0
- output 2: bfloat16 [4, 640, 2560], P('rep'), parts along dimension 0
- output 3: bfloat16 [4, 2560, 640], P('rep'), parts along dimension 0
- output 4: float32 [4, 640, 2560], P('rep', 'dp'), parts along dimension 0
- output 5: float32 [4, 640, 2560], P('rep', 'dp'), parts along dimension 0
- output 6: float32 [4, 2560, 640], P('rep', 'dp'), parts along dimension 0
- output 7: float32 [4, 640, 2560], P('rep', 'dp'), parts along dimension 0
- output 8: float32 [4, 640, 2560], P('rep', 'dp'), parts along dimension 0
- output 9: float32 [4, 2560, 640], P('rep', 'dp'), parts along dimension 0
There are 2 independent parts. A program takes and returns all parts, laid end to end along the dimension named above; an argument that names none is the same for every part.
All inputs are finite; a program needn't handle non-finite values.
Results may differ from a plain program's by a relative error of at most 0.022.
Values are sent between devices in bfloat16 or wider.
A program may use at most 2 GiB of HBM per device.

v0:
```python
import jax
import jax.numpy as jnp
from jax import lax

NAMES = ("w_gate", "w_up", "w_down")


def matmul(a, w):
    return jnp.dot(a, w, preferred_element_type=jnp.float32).astype(jnp.bfloat16)


def normed(h):
    wide = h.astype(jnp.float32)
    scale = lax.rsqrt(jnp.mean(wide**2, -1, keepdims=True) + 1e-6)
    return (wide * scale).astype(jnp.bfloat16)


def layer(h, w):
    a = normed(h)
    gate = jnp.dot(a, w["w_gate"], preferred_element_type=jnp.float32)
    up = jnp.dot(a, w["w_up"], preferred_element_type=jnp.float32)
    return h + matmul((jax.nn.silu(gate) * up).astype(jnp.bfloat16), w["w_down"])


def adamw(w, m, v, g):
    m = 0.9 * m + 0.1 * g
    v = 0.95 * v + 0.05 * g * g
    step = m * lax.rsqrt(v + 1e-8) + 0.1 * w
    return (w - 0.02 * step).astype(jnp.bfloat16), m, v


def clipped(gradients, sum_of_squares, count):
    factor = jnp.minimum(1.0, 0.5 * lax.rsqrt(sum_of_squares / count + 1e-30))
    return [g * factor for g in gradients]


def stack(weights, h):
    for number in range(weights["w_gate"].shape[0]):
        h = layer(h, {name: w[number] for name, w in weights.items()})
    return h


def solution(mesh):
    groups = mesh.shape["rep"]

    def step(x, dy, *arrays):
        weights, m, v = (arrays[i : i + 3] for i in (0, 3, 6))
        x, dy = (t.reshape(groups, -1, *t.shape[1:]) for t in (x, dy))

        def of_a_group(x, dy):
            _, back = jax.vjp(lambda w: stack(w, x), dict(zip(NAMES, weights, strict=True)))
            by_weights = back(dy)[0]
            gradients = [by_weights[name].astype(jnp.float32) for name in NAMES]
            gradients = clipped(gradients, sum(jnp.sum(g * g) for g in gradients), sum(g.size for g in gradients))
            new = [adamw(w.astype(jnp.float32), m, v, g) for w, m, v, g in zip(weights, m, v, gradients, strict=True)]
            return tuple(one[which] for which in range(3) for one in new)

        return tuple(t.reshape(-1, *t.shape[2:]) for t in jax.vmap(of_a_group)(x, dy))

    return step
```

profile of v0, /device:TPU:0, one launch (start us, length us, event | category | flops | bytes accessed | tf_op | source)
XLA Modules:
  0.0 1249.1 jit_solution(7372278359384730909)
XLA Ops:
  17.5 13.4 %convolution_convert_fusion.1 = bf16[2048,2560]{1,0:T(8,128)(2,1)} fusion(bf16[2,2560,640]{2,1,0:T(8,128)(2,1)} %param.16, bf16[1,2048,640]{2,1,0:T(8,128)(2,1)} %param.17), kind=kOutput, calls=%fused_computation.199 | convolution fusion | flops 6716129280 | bytes 16384000 | tf_op jit(solution)/vmap(transpose(jvp()))/dot_general | solution.py:9
  30.9 13.9 %fusion.188 = f32[2048,2560]{1,0:T(8,128)} fusion(bf16[2,640,2560]{2,1,0:T(8,128)(2,1)} %param.12, bf16[1,2048,640]{2,1,0:T(8,128)(2,1)S(1)} %copy-done.15, f32[2048]{0:T(1024)S(1)} %add_rsqrt_fusion), kind=kOutput, calls=%fused_computation.228 | convolution fusion | flops 6714818560 | bytes 26877952 | tf_op jit(solution)/vmap(jvp())/dot_general | solution.py:20
  44.8 22.0 %fusion.164 = (bf16[1,1,2048,2560]{3,2,1,0:T(8,128)(2,1)}, f32[2048,2560]{1,0:T(8,128)}) fusion(f32[2048,2560]{1,0:T(8,128)} %fusion.188, bf16[2,640,2560]{2,1,0:T(8,128)(2,1)} %param.15, bf16[1,2048,640]{2,1,0:T(8,128)(2,1)S(1)} %copy-done.15, f32[2048]{0:T(1024)S(1)} %add_rsqrt_fusion), kind=kOutput, calls=%fused_computation.191 | convolution fusion | flops 6746275840 | bytes 58335232 | tf_op jit(solution)/vmap(jvp())/dot_general | solution.py:21
  66.9 14.5 %copy.4 = bf16[1,1,2048,2560]{2,3,1,0:T(8,128)(2,1)} copy(bf16[1,1,2048,2560]{3,2,1,0:T(8,128)(2,1)} %get-tuple-element.263) | data formatting | bytes 20971520
  81.4 11.4 fusion.174
  94.3 14.4 %fusion.180 = f32[2048,2560]{1,0:T(8,128)} fusion(bf16[2,640,2560]{2,1,0:T(8,128)(2,1)} %param.15, bf16[1,1,2048,640]{2,3,1,0:T(8,128)(2,1)S(1)} %fusion.175), kind=kOutput, calls=%fused_computation.220 | convolution fusion | flops 6710886400 | bytes 26869760 | tf_op jit(solution)/vmap(jvp())/dot_general | solution.py:21
  108.7 28.2 %fusion.153 = (bf16[1,1,2048,2560]{3,2,1,0:T(8,128)(2,1)S(1)}, bf16[1,1,2048,2560]{3,2,1,0:T(8,128)(2,1)}, f32[2048,2560]{1,0:T(8,128)}) fusion(f32[2048,2560]{1,0:T(8,128)} %fusion.180, bf16[2048,2560]{1,0:T(8,128)(2,1)} %convolution_convert_fusion.1, bf16[2,640,2560]{2,1,0:T(8,128)(2,1)} %param.12, bf16[1,1,2048,640]{2,3,1,0:T(8,128)(2,1)S(1)} %fusion.175), kind=kOutput, calls=%fused_computation.175 | convolution fusion | flops 6789529600 | bytes 79298560 | tf_op jit(solution)/vmap(jvp())/dot_general | solution.py:20
  136.9 14.7 %fusion.198 = bf16[2048,640]{0,1:T(8,128)(2,1)S(1)} fusion(bf16[1,1,2048,2560]{3,2,1,0:T(8,128)(2,1)} %get-tuple-element.622, bf16[2,640,2560]{2,1,0:T(8,128)(2,1)} %param.15), kind=kOutput, calls=%fused_computation.234 | convolution fusion | flops 6710886400 | bytes 16384000 | tf_op jit(solution)/vmap(transpose(jvp()))/dot_general | solution.py:21
  151.7 9.1 fusion.176
  167.3 125.9 %while.17 = (bf16[1,1,2048,2560]{2,3,1,0:T(8,128)(2,1)}, bf16[1,1,2048,640]{3,2,1,0:T(8,128)(2,1)S(1)}, f32[1,160,640]{2,1,0:T(8,128)S(1)}, f32[1,160,640]{2,1,0...) while((bf16[1,1,2048,2560]{2,3,1,0:T(8,128)(2,1)}, ...), condition=%wide.windowed_dot_general_cond_rs.5.clone, body=%wide.windowed_dot_general_body_rs.5.clone.sunk | while | flops 1683578880 | bytes 40960612 | solution.py:9
  293.2 19.6 %fusion.163 = bf16[1,1,2048,2560]{3,2,1,0:T(8,128)(2,1)} fusion(f32[2048,2560]{1,0:T(8,128)} %fusion.180, f32[2048,2560]{1,0:T(8,128)} %get-tuple-element.267), kind=kLoop, calls=%fused_computation.189 | loop fusion | flops 31457280 | bytes 52428800 | tf_op jit(solution)/vmap(jvp())/convert_element_type | solution.py:22
  312.8 14.6 %copy.2 = bf16[1,1,2048,2560]{2,3,1,0:T(8,128)(2,1)} copy(bf16[1,1,2048,2560]{3,2,1,0:T(8,128)(2,1)} %fusion.163) | data formatting | bytes 20971520
  330.6 131.2 %while.16 = (bf16[1,1,2048,2560]{2,3,1,0:T(8,128)(2,1)}, bf16[1,1,2048,640]{3,2,1,0:T(8,128)(2,1)S(1)}, f32[1,160,640]{2,1,0:T(8,128)S(1)}, f32[1,160,640]{2,1,0...) while((bf16[1,1,2048,2560]{2,3,1,0:T(8,128)(2,1)}, ...), condition=%wide.windowed_dot_general_cond_rs.4.clone, body=%wide.windowed_dot_general_body_rs.4.clone.sunk | while | flops 1683578880 | bytes 44237468 | solution.py:9
  465.9 28.9 %convert_multiply_fusion = (bf16[1,1,2048,2560]{3,2,1,0:T(8,128)(2,1)}, bf16[1,1,2048,2560]{3,2,1,0:T(8,128)(2,1)}) fusion(f32[2048,2560]{1,0:T(8,128)} %fusion.188, f32[2048,2560]{1,0:T(8,128)} %get-tuple-element.264, bf16[2,2560,640]{2,1,0:T(8,128)(2,1)} %param.16, bf16[1,1,2048,640]{2,3,1,0:T(8,128)(2,1)} %fusion.219), kind=kOutput, calls=%fused_computation.170 | convolution fusion | flops 6794772480 | bytes 68812800 | tf_op jit(solution)/vmap(transpose(jvp()))/dot_general | solution.py:9
  494.8 112.3 %while.15 = (bf16[1,1,2048,640]{2,3,1,0:T(8,128)(2,1)}, bf16[1,1,2048,2560]{3,2,1,0:T(8,128)(2,1)}, f32[1,40,2560]{2,1,0:T(8,128)S(1)}, f32[1,40,2560]{2,1,0:T(8...) while((bf16[1,1,2048,640]{2,3,1,0:T(8,128)(2,1)}, ...), condition=%wide.windowed_dot_general_cond_rs.3.clone, body=%wide.windowed_dot_general_body_rs.3.clone.sunk | while | flops 1679646720 | bytes 82903744 | solution.py:21
  607.9 120.5 %while.14 = (bf16[1,1,2048,640]{2,3,1,0:T(8,128)(2,1)}, bf16[1,1,2048,2560]{3,2,1,0:T(8,128)(2,1)}, f32[1,40,2560]{2,1,0:T(8,128)S(1)}, f32[1,40,2560]{2,1,0:T(8...) while((bf16[1,1,2048,640]{2,3,1,0:T(8,128)(2,1)}, ...), condition=%wide.windowed_dot_general_cond_rs.2.clone, body=%wide.windowed_dot_general_body_rs.2.clone.sunk | while | flops 1679646720 | bytes 82903744 | solution.py:21
  729.1 119.4 %while.13 = (bf16[1,1,2048,640]{2,3,1,0:T(8,128)(2,1)}, bf16[1,1,2048,2560]{3,2,1,0:T(8,128)(2,1)}, f32[1,40,2560]{2,1,0:T(8,128)S(1)}, f32[1,40,2560]{2,1,0:T(8...) while((bf16[1,1,2048,640]{2,3,1,0:T(8,128)(2,1)}, ...), condition=%wide.windowed_dot_general_cond_rs.1.clone, body=%wide.windowed_dot_general_body_rs.1.clone.sunk | while | flops 1679646720 | bytes 82903744 | solution.py:20
  848.5 120.6 %while.12 = (bf16[1,1,2048,640]{2,3,1,0:T(8,128)(2,1)}, bf16[1,1,2048,2560]{3,2,1,0:T(8,128)(2,1)}, f32[1,40,2560]{2,1,0:T(8,128)S(1)}, f32[1,40,2560]{2,1,0:T(8...) while((bf16[1,1,2048,640]{2,3,1,0:T(8,128)(2,1)}, ...), condition=%wide.windowed_dot_general_cond_rs.clone, body=%wide.windowed_dot_general_body_rs.clone.sunk | while | flops 1679646720 | bytes 82903744 | solution.py:20
  971.0 7.0 collective-permute-start.24
  990.9 32.0 %all-reduce.10 = f32[1]{0:T(128)} all-reduce(f32[1]{0:T(128)} %bitcast.39), channel_id=13, replica_groups=mesh['rep'=2,'dp'=16] {'dp'}, use_global_device_ids=true, to_apply=%region_3.4.clone | all-reduce | flops 1 | bytes 8 | tf_op jit(solution)/vmap()/reduce_sum | solution.py:54
  1032.9 65.2 %all-gather.14.cloned.1.call-done = bf16[1,2,2560,640]{3,2,1,0:T(8,128)(2,1)} async-done(((bf16[1,2,160,640]{3,2,1,0:T(8,128)(2,1)}), bf16[1,2,2560,640]{3,2,1,0:T(8,128)(2,1)}) %all-gather.14.cloned.1.call-update) | async-done | bytes 6553616 | tf_op jit(solution)/reshape | solution.py:58
  1098.1 64.9 %all-gather.12.cloned.1.call-done = bf16[1,2,640,2560]{3,2,1,0:T(8,128)(2,1)} async-done(((bf16[1,2,40,2560]{3,2,1,0:T(8,128)(2,1)}), bf16[1,2,640,2560]{3,2,1,0:T(8,128)(2,1)}) %all-gather.12.cloned.1.call-update) | async-done | bytes 6553616 | tf_op jit(solution)/reshape | solution.py:58
  1162.9 64.9 %all-gather.10.cloned.1.call-done = bf16[1,2,640,2560]{3,2,1,0:T(8,128)(2,1)} async-done(((bf16[1,2,40,2560]{3,2,1,0:T(8,128)(2,1)}), bf16[1,2,640,2560]{3,2,1,0:T(8,128)(2,1)}) %all-gather.10.cloned.1.call-update) | async-done | bytes 6553616 | tf_op jit(solution)/reshape | solution.py:58
  1227.8 6.8 copy.63
  (621 shorter events, 739.0 us)
Async XLA Ops:
  7.2 1090.9 %all-gather.14.cloned.1.call-start = ((), (), s32[]{:S(2)}) async-start(), calls=%async_computation.2 | async-start | bytes 6963200 | tf_op jit(solution)/reshape | solution.py:58
  244.0 14.1 %collective-permute-start.22 = (f32[1,160,640]{2,1,0:T(8,128)}, f32[1,160,640]{2,1,0:T(8,128)S(1)}, u32[]{:S(2)}, u32[]{:S(2)}) collective-permute-start(f32[1,160,640]{2,1,0:T(8,128)} %get-tuple-element.500), channel_id=37, source_target_pairs={{0,1},{1,2},{2,3},{3,4},{4,5},{5,6},{6,7},{7,8},{8,9},{9,10},{10,1... | collective-permute-start | bytes 1228808 | tf_op jit(solution)/vmap(transpose(jvp()))/dot_general | solution.py:9
  244.0 14.1 %collective-permute-start.23 = (f32[1,160,640]{2,1,0:T(8,128)S(1)}, f32[1,160,640]{2,1,0:T(8,128)}, u32[]{:S(2)}, u32[]{:S(2)}) collective-permute-start(f32[1,160,640]{2,1,0:T(8,128)S(1)} %get-tuple-element.501), channel_id=36, source_target_pairs={{0,15},{1,0},{2,1},{3,2},{4,3},{5,4},{6,5},{7,6},{8,7},{9,8},{10,9... | collective-permute-start | bytes 1228808 | tf_op jit(solution)/vmap(transpose(jvp()))/dot_general | solution.py:9
  277.1 14.2 %collective-permute-start.23 = (f32[1,160,640]{2,1,0:T(8,128)S(1)}, f32[1,160,640]{2,1,0:T(8,128)}, u32[]{:S(2)}, u32[]{:S(2)}) collective-permute-start(f32[1,160,640]{2,1,0:T(8,128)S(1)} %get-tuple-element.501), channel_id=36, source_target_pairs={{0,15},{1,0},{2,1},{3,2},{4,3},{5,4},{6,5},{7,6},{8,7},{9,8},{10,9... | collective-permute-start | bytes 1228808 | tf_op jit(solution)/vmap(transpose(jvp()))/dot_general | solution.py:9
  293.2 677.8 %collective-permute-start.29 = (f32[1,160,640]{2,1,0:T(8,128)}, f32[1,160,640]{2,1,0:T(8,128)}, u32[]{:S(2)}, u32[]{:S(2)}) collective-permute-start(f32[1,160,640]{2,1,0:T(8,128)} %get-tuple-element.47), channel_id=38, source_target_pairs={{0,1},{1,2},{2,3},{3,4},{4,5},{5,6},{6,7},{7,8},{8,9},{9,10},{10,1... | collective-permute-start | bytes 1228808 | tf_op jit(solution)/vmap(transpose(jvp()))/dot_general | solution.py:9
  345.5 14.7 %collective-permute-start.19 = (f32[1,160,640]{2,1,0:T(8,128)S(1)}, f32[1,160,640]{2,1,0:T(8,128)}, u32[]{:S(2)}, u32[]{:S(2)}) collective-permute-start(f32[1,160,640]{2,1,0:T(8,128)S(1)} %get-tuple-element.492), channel_id=30, source_target_pairs={{0,15},{1,0},{2,1},{3,2},{4,3},{5,4},{6,5},{7,6},{8,7},{9,8},{10,9... | collective-permute-start | bytes 1228808 | tf_op jit(solution)/vmap(transpose(jvp()))/dot_general | solution.py:9
  411.4 14.7 %collective-permute-start.19 = (f32[1,160,640]{2,1,0:T(8,128)S(1)}, f32[1,160,640]{2,1,0:T(8,128)}, u32[]{:S(2)}, u32[]{:S(2)}) collective-permute-start(f32[1,160,640]{2,1,0:T(8,128)S(1)} %get-tuple-element.492), channel_id=30, source_target_pairs={{0,15},{1,0},{2,1},{3,2},{4,3},{5,4},{6,5},{7,6},{8,7},{9,8},{10,9... | collective-permute-start | bytes 1228808 | tf_op jit(solution)/vmap(transpose(jvp()))/dot_general | solution.py:9
  444.9 14.1 %collective-permute-start.18 = (f32[1,160,640]{2,1,0:T(8,128)}, f32[1,160,640]{2,1,0:T(8,128)S(1)}, u32[]{:S(2)}, u32[]{:S(2)}) collective-permute-start(f32[1,160,640]{2,1,0:T(8,128)} %get-tuple-element.491), channel_id=31, source_target_pairs={{0,1},{1,2},{2,3},{3,4},{4,5},{5,6},{6,7},{7,8},{8,9},{9,10},{10,1... | collective-permute-start | bytes 1228808 | tf_op jit(solution)/vmap(transpose(jvp()))/dot_general | solution.py:9
  444.9 14.8 %collective-permute-start.19 = (f32[1,160,640]{2,1,0:T(8,128)S(1)}, f32[1,160,640]{2,1,0:T(8,128)}, u32[]{:S(2)}, u32[]{:S(2)}) collective-permute-start(f32[1,160,640]{2,1,0:T(8,128)S(1)} %get-tuple-element.492), channel_id=30, source_target_pairs={{0,15},{1,0},{2,1},{3,2},{4,3},{5,4},{6,5},{7,6},{8,7},{9,8},{10,9... | collective-permute-start | bytes 1228808 | tf_op jit(solution)/vmap(transpose(jvp()))/dot_general | solution.py:9
  461.8 517.3 %collective-permute-start.28 = (f32[1,160,640]{2,1,0:T(8,128)}, f32[1,160,640]{2,1,0:T(8,128)}, u32[]{:S(2)}, u32[]{:S(2)}) collective-permute-start(f32[1,160,640]{2,1,0:T(8,128)} %get-tuple-element.45), channel_id=32, source_target_pairs={{0,1},{1,2},{2,3},{3,4},{4,5},{5,6},{6,7},{7,8},{8,9},{9,10},{10,1... | collective-permute-start | bytes 1228808 | tf_op jit(solution)/vmap(transpose(jvp()))/dot_general | solution.py:9
  494.8 14.1 %collective-permute-start.12 = (f32[1,40,2560]{2,1,0:T(8,128)S(1)}, f32[1,40,2560]{2,1,0:T(8,128)S(1)}, u32[]{:S(2)}, u32[]{:S(2)}) collective-permute-start(f32[1,40,2560]{2,1,0:T(8,128)S(1)} %broadcast_select_fusion.30), channel_id=22, source_target_pairs={{0,1},{1,2},{2,3},{3,4},{4,5},{5,6},{6,7},{7,8},{8,9},{9,10},{10,1... | collective-permute-start | bytes 1228808 | tf_op jit(solution)/vmap(transpose(jvp()))/dot_general | solution.py:21
  580.0 14.1 %collective-permute-start.12 = (f32[1,40,2560]{2,1,0:T(8,128)S(1)}, f32[1,40,2560]{2,1,0:T(8,128)S(1)}, u32[]{:S(2)}, u32[]{:S(2)}) collective-permute-start(f32[1,40,2560]{2,1,0:T(8,128)S(1)} %broadcast_select_fusion.30), channel_id=22, source_target_pairs={{0,1},{1,2},{2,3},{3,4},{4,5},{5,6},{6,7},{7,8},{8,9},{9,10},{10,1... | collective-permute-start | bytes 1228808 | tf_op jit(solution)/vmap(transpose(jvp()))/dot_general | solution.py:21
  607.1 374.0 %collective-permute-start.27 = (f32[1,40,2560]{2,1,0:T(8,128)}, f32[1,40,2560]{2,1,0:T(8,128)}, u32[]{:S(2)}, u32[]{:S(2)}) collective-permute-start(f32[1,40,2560]{2,1,0:T(8,128)} %get-tuple-element.43), channel_id=25, source_target_pairs={{0,1},{1,2},{2,3},{3,4},{4,5},{5,6},{6,7},{7,8},{8,9},{9,10},{10,1... | collective-permute-start | bytes 1228808 | tf_op jit(solution)/vmap(transpose(jvp()))/dot_general | solution.py:21
  608.9 17.1 %collective-permute-start.8 = (f32[1,40,2560]{2,1,0:T(8,128)}, f32[1,40,2560]{2,1,0:T(8,128)}, u32[]{:S(2)}, u32[]{:S(2)}) collective-permute-start(f32[1,40,2560]{2,1,0:T(8,128)} %broadcast_select_fusion.28), channel_id=16, source_target_pairs={{0,1},{1,2},{2,3},{3,4},{4,5},{5,6},{6,7},{7,8},{8,9},{9,10},{10,1... | collective-permute-start | bytes 1228808 | tf_op jit(solution)/vmap(transpose(jvp()))/dot_general | solution.py:21
  609.7 16.3 %collective-permute-start.9 = (f32[1,40,2560]{2,1,0:T(8,128)}, f32[1,40,2560]{2,1,0:T(8,128)S(1)}, u32[]{:S(2)}, u32[]{:S(2)}) collective-permute-start(f32[1,40,2560]{2,1,0:T(8,128)} %broadcast_select_fusion.29), channel_id=15, source_target_pairs={{0,15},{1,0},{2,1},{3,2},{4,3},{5,4},{6,5},{7,6},{8,7},{9,8},{10,9... | collective-permute-start | bytes 1228808 | tf_op jit(solution)/vmap(transpose(jvp()))/dot_general | solution.py:21
  700.3 14.2 %collective-permute-start.8 = (f32[1,40,2560]{2,1,0:T(8,128)}, f32[1,40,2560]{2,1,0:T(8,128)}, u32[]{:S(2)}, u32[]{:S(2)}) collective-permute-start(f32[1,40,2560]{2,1,0:T(8,128)} %broadcast_select_fusion.28), channel_id=16, source_target_pairs={{0,1},{1,2},{2,3},{3,4},{4,5},{5,6},{6,7},{7,8},{8,9},{9,10},{10,1... | collective-permute-start | bytes 1228808 | tf_op jit(solution)/vmap(transpose(jvp()))/dot_general | solution.py:21
  729.9 14.2 %collective-permute-start.4 = (f32[1,40,2560]{2,1,0:T(8,128)}, f32[1,40,2560]{2,1,0:T(8,128)}, u32[]{:S(2)}, u32[]{:S(2)}) collective-permute-start(f32[1,40,2560]{2,1,0:T(8,128)} %broadcast_select_fusion.26), channel_id=9, source_target_pairs={{0,1},{1,2},{2,3},{3,4},{4,5},{5,6},{6,7},{7,8},{8,9},{9,10},{10,1... | collective-permute-start | bytes 1228808 | tf_op jit(solution)/vmap(transpose(jvp()))/dot_general | solution.py:20
  759.9 14.2 %collective-permute-start.4 = (f32[1,40,2560]{2,1,0:T(8,128)}, f32[1,40,2560]{2,1,0:T(8,128)}, u32[]{:S(2)}, u32[]{:S(2)}) collective-permute-start(f32[1,40,2560]{2,1,0:T(8,128)} %broadcast_select_fusion.26), channel_id=9, source_target_pairs={{0,1},{1,2},{2,3},{3,4},{4,5},{5,6},{6,7},{7,8},{8,9},{9,10},{10,1... | collective-permute-start | bytes 1228808 | tf_op jit(solution)/vmap(transpose(jvp()))/dot_general | solution.py:20
  789.9 14.3 %collective-permute-start.4 = (f32[1,40,2560]{2,1,0:T(8,128)}, f32[1,40,2560]{2,1,0:T(8,128)}, u32[]{:S(2)}, u32[]{:S(2)}) collective-permute-start(f32[1,40,2560]{2,1,0:T(8,128)} %broadcast_select_fusion.26), channel_id=9, source_target_pairs={{0,1},{1,2},{2,3},{3,4},{4,5},{5,6},{6,7},{7,8},{8,9},{9,10},{10,1... | collective-permute-start | bytes 1228808 | tf_op jit(solution)/vmap(transpose(jvp()))/dot_general | solution.py:20
  820.2 14.3 %collective-permute-start.4 = (f32[1,40,2560]{2,1,0:T(8,128)}, f32[1,40,2560]{2,1,0:T(8,128)}, u32[]{:S(2)}, u32[]{:S(2)}) collective-permute-start(f32[1,40,2560]{2,1,0:T(8,128)} %broadcast_select_fusion.26), channel_id=9, source_target_pairs={{0,1},{1,2},{2,3},{3,4},{4,5},{5,6},{6,7},{7,8},{8,9},{9,10},{10,1... | collective-permute-start | bytes 1228808 | tf_op jit(solution)/vmap(transpose(jvp()))/dot_general | solution.py:20
  909.9 14.1 %collective-permute-start = (f32[1,40,2560]{2,1,0:T(8,128)}, f32[1,40,2560]{2,1,0:T(8,128)}, u32[]{:S(2)}, u32[]{:S(2)}) collective-permute-start(f32[1,40,2560]{2,1,0:T(8,128)} %broadcast_select_fusion.24), channel_id=3, source_target_pairs={{0,1},{1,2},{2,3},{3,4},{4,5},{5,6},{6,7},{7,8},{8,9},{9,10},{10,1... | collective-permute-start | bytes 1228808 | tf_op jit(solution)/vmap(transpose(jvp()))/dot_general | solution.py:20
  971.0 17.1 %collective-permute-start.24 = (f32[1,40,2560]{2,1,0:T(8,128)}, f32[1,40,2560]{2,1,0:T(8,128)S(1)}, u32[]{:S(2)}, u32[]{:S(2)}) collective-permute-start(f32[1,40,2560]{2,1,0:T(8,128)} %get-tuple-element.37), channel_id=6, source_target_pairs={{0,1},{1,2},{2,3},{3,4},{4,5},{5,6},{6,7},{7,8},{8,9},{9,10},{10,1... | collective-permute-start | bytes 1228808 | tf_op jit(solution)/vmap(transpose(jvp()))/dot_general | solution.py:20
  1026.6 136.3 %all-gather.12.cloned.1.call-start = ((), (), s32[]{:S(2)}) async-start(), calls=%async_computation.1 | async-start | bytes 6963200 | tf_op jit(solution)/reshape | solution.py:58
  1030.0 197.8 %all-gather.10.cloned.1.call-start = ((), (), s32[]{:S(2)}) async-start(), calls=%async_computation | async-start | bytes 6963200 | tf_op jit(solution)/reshape | solution.py:58
  (175 other events, 2546.8 us)
Sparse Core Ops, SparseCore 0:
  1026.8 71.2 all-gather.13
  1100.9 62.0 all-gather.11
  1165.8 62.0 all-gather.9
where the time goes:
time: 1260 us; the launch traced here: 1250 us
  waiting for transfers between devices  363 us (29%)
  matrix products  326 us (26%)
  starting transfers between devices  224 us (18%)
  other arithmetic  159 us (13%)
  local copies, waits for them, and re-layouts  81.1 us (6%)
  loops' own time  46.9 us (4%)
  blocking collectives  32 us (3%)
  between operations  17.8 us (1%)
    reshape x3, waiting for transfers between devices, step(): t.reshape(-1, *t.shape[2:])  195 us
    dot_general x19, matrix products, layer(): gate = jnp.dot(a, w['w_gate'], preferred_element_type=jnp.float32)  116 us
    dot_general x19, matrix products, layer(): up = jnp.dot(a, w['w_up'], preferred_element_type=jnp.float32)  116 us
    dot_general x19, matrix products, matmul(): jnp.dot(a, w, preferred_element_type=jnp.float32).astype(jnp.bfloat16)  93.1 us
    dot_general x34, starting transfers between devices, layer(): gate = jnp.dot(a, w['w_gate'], preferred_element_type=jnp.float32)  79.3 us
    dot_general x34, starting transfers between devices, matmul(): jnp.dot(a, w, preferred_element_type=jnp.float32).astype(jnp.bfloat16)  72.9 us
    dot_general x34, starting transfers between devices, layer(): up = jnp.dot(a, w['w_up'], preferred_element_type=jnp.float32)  71.6 us
    dot_general x34, waiting for transfers between devices, matmul(): jnp.dot(a, w, preferred_element_type=jnp.float32).astype(jnp.bfloat16)  69.3 us
  transfers between devices with their start and end apart: 105, of which 47 were waited for; matrix products, arithmetic and copies ran while one was open for 29% of the time, Pallas kernels for 0%

commit v1 on v0

v1 whole, which is shorter than its diff:
```python
import functools

import jax
import jax.numpy as jnp
from jax import lax
from jax.experimental import pallas as pl
from jax.experimental.pallas import tpu as pltpu
from jax.sharding import PartitionSpec as P

F32, BF16 = jnp.float32, jnp.bfloat16
MESH = pl.DeviceIdType.MESH


def matmul(a, w):
    return jnp.dot(a, w, preferred_element_type=F32).astype(BF16)


def normed(h):
    wide = h.astype(F32)
    scale = lax.rsqrt(jnp.mean(wide**2, -1, keepdims=True) + 1e-6)
    return (wide * scale).astype(BF16)


def layer(h, wg, wu, wd):
    a = normed(h)
    gate = jnp.dot(a, wg, preferred_element_type=F32)
    up = jnp.dot(a, wu, preferred_element_type=F32)
    return h + matmul((jax.nn.silu(gate) * up).astype(BF16), wd)


def ring(p):
    return p + (p // 4) * (11 - 2 * p)


def comm_kernel(count, *refs):
    dw, w, m, v = refs[0:6], refs[6:9], refs[9:12], refs[12:15]
    w_out, m_out, v_out = refs[15:18], refs[18:21], refs[21:24]
    (og, od, pg, pd, rg, rd, mg, md, vg, vd, wg, wd, sums,
     load_sem, half_send, half_recv, rs_send, rs_recv, sum_send, sum_recv,
     ag_send, ag_recv, d2d_send, d2d_recv, store_sem) = refs[24:]
    items = [(0, 0), (1, 0), (2, 0), (0, 1), (1, 1), (2, 1)]

    def at(k, big, small):
        which, layer_ = items[k]
        return small.at[layer_] if which == 2 else big.at[2 * layer_ + which]

    rep, dp = lax.axis_index("rep"), lax.axis_index("dp")
    chip, core = dp // 2, dp % 2
    place = ring(chip)
    way = 1 - 2 * core
    to = 2 * ring((place + way + 8) % 8) + core
    partner = dp + way

    barrier = pltpu.get_barrier_semaphore()
    for off in range(1, 16):
        pl.semaphore_signal(barrier, inc=1, device_id=(rep, (dp + off) % 16), device_id_type=MESH)

    loads = []
    for k, (which, layer_) in enumerate(items):
        for n, (src, dst) in enumerate((
            (dw[k].at[:, core], at(k, og, od)),
            (m[which].at[layer_], at(k, mg, md)),
            (v[which].at[layer_], at(k, vg, vd)),
            (w[which].at[layer_, dp], at(k, wg, wd)),
        )):
            c = pltpu.make_async_copy(src, dst, load_sem.at[k, n])
            c.start()
            loads.append(c)
    pl.semaphore_wait(barrier, 15)

    def remote(src, dst, s, r, device):
        return pltpu.make_async_remote_copy(
            src_ref=src, dst_ref=dst, send_sem=s, recv_sem=r, device_id=(rep, device), device_id_type=MESH)

    halves = []
    for k in range(6):
        c = remote(dw[k].at[:, 1 - core], at(k, pg, pd), half_send.at[k], half_recv.at[k], partner)
        c.start()
        halves.append(c)
    for c in loads:
        c.wait()

    def owner(s):
        return ring((place - way * (1 + s) + 16) % 8)

    def ring_copy(k, s, src):
        return remote(src, at(k, rg, rd).at[s], rs_send.at[k, s], rs_recv.at[k, s], to)

    for k in range(6):
        halves[k].wait_recv()
        mine = at(k, og, od).at[owner(0)]
        mine[...] = (mine[...].astype(F32) + at(k, pg, pd).at[owner(0)][...].astype(F32)).astype(BF16)
        ring_copy(k, 0, mine).start()

    def total(k, s):
        who = owner(s + 1)
        return at(k, rg, rd).at[s][...].astype(F32) + (
            at(k, og, od).at[who][...].astype(F32) + at(k, pg, pd).at[who][...].astype(F32))

    def hop(s, _):
        for k in range(6):
            slot = at(k, rg, rd).at[s]
            ring_copy(k, s, slot).wait_recv()
            slot[...] = total(k, s).astype(BF16)
            ring_copy(k, s + 1, slot).start()
        return _

    lax.fori_loop(0, 6, hop, 0)

    squares = jnp.zeros((8, 128), F32)
    for k in range(6):
        slot = at(k, rg, rd).at[6]
        ring_copy(k, 6, slot).wait_recv()
        g = total(k, 6).astype(BF16)
        slot[...] = g
        g = g.astype(F32)
        g = g * g
        part = g[0:8]
        for i in range(1, g.shape[0] // 8):
            part = part + g[8 * i : 8 * i + 8]
        for i in range(part.shape[1] // 128):
            squares = squares + part[:, 128 * i : 128 * i + 128]
    sums.at[dp][...] = squares

    def sum_copy(off):
        return remote(sums.at[dp], sums.at[dp], sum_send.at[off], sum_recv.at[off], (dp + off) % 16)

    for off in range(1, 16):
        sum_copy(off).start()
    for off in range(1, 16):
        sum_copy(off).wait_recv()
    mean = jnp.sum(sums[...]) / count
    factor = jnp.minimum(1.0, 0.5 * lax.rsqrt(jnp.full((8, 128), mean + 1e-30, F32)))[0:1, 0:1]

    def gather_copy(k, s, who):
        which, layer_ = items[k]
        block = w_out[which].at[layer_, who]
        src = at(k, wg, wd) if isinstance(s, int) and s == 0 else block
        return remote(src, block, ag_send.at[k, s], ag_recv.at[k, s], to)

    def d2d_copy(k, s, who):
        which, layer_ = items[k]
        block = w_out[which].at[layer_, who]
        src = at(k, wg, wd) if isinstance(s, int) and s == 0 else block
        return remote(src, block, d2d_send.at[k, s], d2d_recv.at[k, s], partner)

    stores = []
    for k, (which, layer_) in enumerate(items):
        g = at(k, rg, rd).at[6][...].astype(F32) * factor
        mk, vk, wk = at(k, mg, md), at(k, vg, vd), at(k, wg, wd)
        new_m = 0.9 * mk[...] + 0.1 * g
        new_v = 0.95 * vk[...] + 0.05 * g * g
        wide = wk[...].astype(F32)
        wk[...] = (wide - 0.02 * (new_m * lax.rsqrt(new_v + 1e-8) + 0.1 * wide)).astype(BF16)
        mk[...] = new_m
        vk[...] = new_v
        gather_copy(k, 0, dp).start()
        d2d_copy(k, 0, dp).start()
        for n, (src, dst) in enumerate((
            (wk, w_out[which].at[layer_, dp]),
            (mk, m_out[which].at[layer_]),
            (vk, v_out[which].at[layer_]),
        )):
            c = pltpu.make_async_copy(src, dst, store_sem.at[k, n])
            c.start()
            stores.append(c)

    def source(s):
        return 2 * ring((place - way * (1 + s) + 16) % 8) + core

    def gather(s, _):
        for k in range(6):
            who = source(s)
            gather_copy(k, s, who).wait_recv()
            gather_copy(k, s + 1, who).start()
            d2d_copy(k, s + 1, who).start()
        return _

    lax.fori_loop(0, 6, gather, 0)
    for k in range(6):
        who = source(6)
        gather_copy(k, 6, who).wait_recv()
        d2d_copy(k, 7, who).start()

    for c in stores:
        c.wait()
    for k in range(6):
        halves[k].wait_send()
    for off in range(1, 16):
        sum_copy(off).wait_send()

    def drain(s, _):
        for k in range(6):
            ring_copy(k, s, at(k, rg, rd).at[s]).wait_send()
            gather_copy(k, s, dp).wait_send()
            d2d_copy(k, s, dp).wait_send()
            d2d_copy(k, s, dp).wait_recv()
        return _

    lax.fori_loop(0, 7, drain, 0)
    for k in range(6):
        d2d_copy(k, 7, dp).wait_send()
        d2d_copy(k, 7, dp).wait_recv()


def comm(count, grads, weights, m, v):
    G, D = (40, 2560), (160, 640)
    any_ = pl.BlockSpec(memory_space=pl.ANY)
    dma = pltpu.SemaphoreType.DMA

    def two(dtype, lead):
        return [pltpu.VMEM((4, *lead, *G), dtype), pltpu.VMEM((2, *lead, *D), dtype)]

    outs = pl.pallas_call(
        functools.partial(comm_kernel, count),
        out_shape=[
            *(jax.ShapeDtypeStruct(t.shape, BF16) for t in weights),
            *(jax.ShapeDtypeStruct(t.shape, F32) for t in (*m, *v)),
        ],
        in_specs=[any_] * 15,
        out_specs=[any_] * 9,
        scratch_shapes=[
            *two(BF16, (8,)), *two(BF16, (8,)), *two(BF16, (7,)),
            *two(F32, ()), *two(F32, ()), *two(BF16, ()),
            pltpu.VMEM((16, 8, 128), F32),
            dma((6, 4)), dma((6,)), dma((6,)), dma((6, 7)), dma((6, 7)), dma((16,)), dma((16,)),
            dma((6, 7)), dma((6, 7)), dma((6, 8)), dma((6, 8)), dma((6, 3)),
        ],
        compiler_params=pltpu.CompilerParams(
            collective_id=0, has_side_effects=True, vmem_limit_bytes=56 * 1024 * 1024),
    )(*grads, *weights, *m, *v)
    return outs


def solution(mesh):
    def body(x, dy, *arrays):
        weights, m, v = (arrays[i : i + 3] for i in (0, 3, 6))
        x, dy = x[0], dy[0]
        split = [tuple(w[n] for w in weights) for n in range(2)]

        def stack(split):
            h = x
            for one in split:
                h = layer(h, *one)
            return h

        by = jax.vjp(stack, split)[1](dy)[0]
        grads = [g.reshape(8, 2, -1, g.shape[-1]) for one in by for g in one]
        blocks = [w.reshape(2, 16, -1, w.shape[-1]) for w in weights]
        count = float(sum(w.size for w in weights))
        out = comm(count, grads, blocks, m, v)
        return (*(o.reshape(w.shape) for o, w in zip(out[:3], weights)), *out[3:])

    whole, rows = P(None, None, None), P(None, "dp", None)
    return jax.shard_map(
        body,
        mesh=mesh,
        in_specs=(P(("rep", "dp"), None, None),) * 2 + (whole,) * 3 + (rows,) * 6,
        out_specs=(P("rep", None, None),) * 3 + (P("rep", "dp", None),) * 6,
        check_vma=False,
    )
```

time: 1260 us -> 490 us (0.39)
  waiting for transfers between devices: 363 us -> 0 us
  starting transfers between devices: 224 us -> 0 us
  Pallas kernels: 0 us -> 208 us
  other arithmetic: 159 us -> 5.05 us
  matrix products: 326 us -> 241 us
  local copies, waits for them, and re-layouts: 81.1 us -> 26.3 us
  loops' own time: 46.9 us -> 0 us
  blocking collectives: 32 us -> 0 us
  between operations: 17.8 us -> 1.34 us
    dot_general x102 -> x0, starting transfers between devices: 224 us -> none  [the longest x34 79.3 us: layer(): gate = jnp.dot(a, w['w_gate'], preferred_element_type=jnp.float32)]
    pallas_call x0 -> x1, Pallas kernels: none -> 208 us  [comm(): pl.pallas_call(functools.partial(comm_kernel, count), out_shape=[*(jax.Sh...]
    reshape x3 -> x0, waiting for transfers between devices: 195 us -> none  [step(): t.reshape(-1, *t.shape[2:])]
    dot_general x102 -> x0, waiting for transfers between devices: 168 us -> none  [the longest x34 69.3 us: matmul(): jnp.dot(a, w, preferred_element_type=jnp.float32).astype(jnp.bfloat16)]
    dot_general x112 -> x0, other arithmetic: 113 us -> none
    dot_general x57 -> x15, matrix products: 326 us -> 241 us  [the longest x5 89.2 us: layer(): gate = jnp.dot(a, wg, preferred_element_type=F32)]
    another operation x6 -> x0, loops' own time: 46.9 us -> none  [the longest x2 15.9 us: matmul(): jnp.dot(a, w, preferred_element_type=jnp.float32).astype(jnp.bfloat16)]
    unnamed x53 -> x59, local copies, waits for them, and re-layouts: 59.9 us -> 26.3 us
  transfers between devices with their start and end apart: 105 -> 0, of which waited for: 47 -> 0; matrix products, arithmetic and copies ran while one was open for 29% -> 0% of each run, Pallas kernels for 0% -> 0%
where the time goes in v1:
time: 490 us; the launch traced here: 481 us
  matrix products  241 us (49%)
  Pallas kernels  208 us (42%)
  local copies, waits for them, and re-layouts  26.3 us (5%)
  other arithmetic  5.05 us (1%)
    pallas_call x1, Pallas kernels, comm(): pl.pallas_call(functools.partial(comm_kernel, count), out_shape=[*(jax.Sh...  208 us
    dot_general x5, matrix products, layer(): gate = jnp.dot(a, wg, preferred_element_type=F32)  89.2 us
    dot_general x5, matrix products, layer(): up = jnp.dot(a, wu, preferred_element_type=F32)  84 us
    dot_general x5, matrix products, matmul(): return jnp.dot(a, w, preferred_element_type=F32).astype(BF16)  67.7 us
    unnamed x59, local copies, waits for them, and re-layouts  26.3 us

profile of v1, /device:TPU:0, one launch (start us, length us, event | category | flops | bytes accessed | tf_op | source)
XLA Modules:
  0.0 481.4 jit_solution(16463381719794093388)
XLA Ops:
  0.6 3.0 copy.20
  4.3 16.1 %fusion.42 = f32[2048,2560]{1,0:T(8,128)} fusion(bf16[2,640,2560]{2,1,0:T(8,128)(2,1)} %param.13, bf16[1,2048,640]{2,1,0:T(8,128)(2,1)} %param.11, f32[2048]{0:T(1024)S(1)} %add_rsqrt_fusion), kind=kOutput, calls=%fused_computation.60 | convolution fusion | flops 6714818560 | bytes 26877952 | tf_op jit(solution)/shard_map/jvp()/dot_general | solution.py:26
  20.4 21.4 %multiply_convert_fusion.1 = (bf16[2048,2560]{1,0:T(8,128)(2,1)}, f32[2048,2560]{1,0:T(8,128)}) fusion(f32[2048,2560]{1,0:T(8,128)} %fusion.42, bf16[2,640,2560]{2,1,0:T(8,128)(2,1)S(1)} %bitcast.90, bf16[1,2048,640]{2,1,0:T(8,128)(2,1)} %param.11, f32[2048]{0:T(1024)S(1)} %add_rsqrt_fusion), kind=kOutput, calls=%fused_computation.17 | convolution fusion | flops 6746275840 | bytes 58335232 | tf_op jit(solution)/shard_map/jvp()/dot_general | solution.py:27
  41.8 11.0 %fusion.19 = (f32[2048]{0:T(1024)S(1)}, bf16[2048,640]{0,1:T(8,128)(2,1)S(1)}) fusion(bf16[2048,2560]{1,0:T(8,128)(2,1)} %get-tuple-element.27, bf16[2,2560,640]{2,1,0:T(8,128)(2,1)} %param.15, bf16[1,2048,640]{1,2,0:T(8,128)(2,1)S(1)} %copy.20), kind=kOutput, calls=%fused_computation.37 | convolution fusion | flops 6717437952 | bytes 19013632 | tf_op jit(solution)/shard_map/jvp()/dot_general | solution.py:15
  52.9 11.8 %fusion.29 = f32[2048,2560]{1,0:T(8,128)} fusion(bf16[2,640,2560]{2,1,0:T(8,128)(2,1)S(1)} %bitcast.90, bf16[2048,640]{0,1:T(8,128)(2,1)S(1)} %get-tuple-element.30, f32[2048]{0:T(1024)S(1)} %fusion.79), kind=kOutput, calls=%fused_computation.47 | convolution fusion | flops 6714818560 | bytes 26877952 | tf_op jit(solution)/shard_map/jvp()/dot_general | solution.py:27
  64.7 12.5 %convolution_convert_fusion.1 = bf16[2048,2560]{1,0:T(8,128)(2,1)} fusion(bf16[2,2560,640]{2,1,0:T(8,128)(2,1)} %param.15, bf16[1,2048,640]{2,1,0:T(8,128)(2,1)S(1)} %copy-done.4), kind=kOutput, calls=%fused_computation.23 | convolution fusion | flops 6716129280 | bytes 16384000 | tf_op jit(solution)/shard_map/transpose(jvp())/dot_general | solution.py:15
  77.2 31.3 %fusion.2 = (bf16[2048,2560]{1,0:T(8,128)(2,1)}, f32[2048,2560]{1,0:T(8,128)}) fusion(f32[2048,2560]{1,0:T(8,128)} %fusion.29, bf16[2048,2560]{1,0:T(8,128)(2,1)} %convolution_convert_fusion.1, bf16[2,640,2560]{2,1,0:T(8,128)(2,1)} %param.13, bf16[2048,640]{0,1:T(8,128)(2,1)} %copy-done.3, f32[2048]{0:T(1024)S(1)} %fusion.79), kind=kOutput, calls=%fused_computation.8 | convolution fusion | flops 6777733120 | bytes 68820992 | tf_op jit(solution)/shard_map/jvp()/dot_general | solution.py:26
  108.5 20.5 %fusion.22 = bf16[2560,640]{1,0:T(8,128)(2,1)} fusion(f32[2048,2560]{1,0:T(8,128)} %fusion.29, bf16[1,2048,640]{2,1,0:T(8,128)(2,1)} %param.12, f32[2048,2560]{1,0:T(8,128)} %get-tuple-element.32), kind=kOutput, calls=%fused_computation.41 | convolution fusion | flops 6743982080 | bytes 47841280 | tf_op jit(solution)/shard_map/transpose(jvp())/dot_general | solution.py:15
  129.0 16.2 %fusion.23 = bf16[640,2560]{1,0:T(8,128)(2,1)} fusion(bf16[2048,2560]{1,0:T(8,128)(2,1)} %convolution_convert_fusion.1, bf16[2048,640]{0,1:T(8,128)(2,1)} %copy-done.3, f32[2048]{0:T(1024)S(1)} %fusion.79, f32[2048,2560]{1,0:T(8,128)} %get-tuple-element.32), kind=kOutput, calls=%fused_computation.42 | convolution fusion | flops 6747914240 | bytes 37363712 | tf_op jit(solution)/shard_map/transpose(jvp())/dot_general | solution.py:27
  145.1 11.8 %convolution_convert_fusion.2 = bf16[640,2560]{1,0:T(8,128)(2,1)} fusion(bf16[2048,2560]{1,0:T(8,128)(2,1)} %get-tuple-element.31, bf16[2048,640]{0,1:T(8,128)(2,1)} %copy-done.3, f32[2048]{0:T(1024)S(1)} %fusion.79), kind=kOutput, calls=%fused_computation.44 | convolution fusion | flops 6714818560 | bytes 16392192 | tf_op jit(solution)/shard_map/transpose(jvp())/dot_general | solution.py:26
  157.0 8.4 %fusion.50 = bf16[2048,640]{0,1:T(8,128)(2,1)} fusion(bf16[2048,2560]{1,0:T(8,128)(2,1)S(1)} %copy-done.15, bf16[2,640,2560]{2,1,0:T(8,128)(2,1)S(1)} %bitcast.87), kind=kOutput, calls=%fused_computation.66 | convolution fusion | flops 6710886400 | bytes 16384000 | tf_op jit(solution)/shard_map/transpose(jvp())/dot_general | solution.py:26
  165.4 19.1 %fusion.21 = (f32[2048]{0:T(1024)S(1)}, bf16[2048,640]{0,1:T(8,128)(2,1)}) fusion(bf16[2048,640]{0,1:T(8,128)(2,1)} %copy-done.3, bf16[2048,640]{0,1:T(8,128)(2,1)} %fusion.50, bf16[2,640,2560]{2,1,0:T(8,128)(2,1)} %param.14, bf16[2048,2560]{1,0:T(8,128)(2,1)} %convolution_convert_fusion.1, f32[2048,2560]{1,0:T(8,128)} %get-tuple-element.32), kind=kOutput, calls=%fused_computation.39 | convolution fusion | flops 6750205952 | bytes 42606592 | tf_op jit(solution)/shard_map/transpose(jvp())/dot_general | solution.py:27
  184.5 3.0 copy.21
  187.5 4.5 fusion.63
  192.0 12.6 %convolution_convert_fusion.3 = bf16[2560,640]{1,0:T(8,128)(2,1)} fusion(bf16[2048,2560]{1,0:T(8,128)(2,1)} %get-tuple-element.27, bf16[2048,640]{0,1:T(8,128)(2,1)S(1)} %fusion.63), kind=kOutput, calls=%fused_computation.45 | convolution fusion | flops 6712524800 | bytes 16384000 | tf_op jit(solution)/shard_map/transpose(jvp())/dot_general | solution.py:15
  204.6 11.1 %convolution_convert_fusion = bf16[2048,2560]{1,0:T(8,128)(2,1)} fusion(bf16[2048,640]{0,1:T(8,128)(2,1)S(1)} %fusion.63, bf16[2,2560,640]{2,1,0:T(8,128)(2,1)S(1)} %bitcast.93), kind=kOutput, calls=%fused_computation.22 | convolution fusion | flops 6716129280 | bytes 16384000 | tf_op jit(solution)/shard_map/transpose(jvp())/dot_general | solution.py:15
  215.8 15.5 %fusion.24 = bf16[640,2560]{1,0:T(8,128)(2,1)} fusion(bf16[2048,2560]{1,0:T(8,128)(2,1)} %convolution_convert_fusion, f32[2048,2560]{1,0:T(8,128)} %fusion.42, bf16[1,2048,640]{1,2,0:T(8,128)(2,1)S(1)} %copy-done.1, f32[2048]{0:T(1024)S(1)} %copy-done.14), kind=kOutput, calls=%fused_computation.43 | convolution fusion | flops 6747914240 | bytes 37363712 | tf_op jit(solution)/shard_map/transpose(jvp())/dot_general | solution.py:27
  231.3 21.7 %fusion.25 = bf16[640,2560]{1,0:T(8,128)(2,1)} fusion(f32[2048,2560]{1,0:T(8,128)} %fusion.42, f32[2048,2560]{1,0:T(8,128)} %get-tuple-element.28, bf16[2048,2560]{1,0:T(8,128)(2,1)} %convolution_convert_fusion, bf16[1,2048,640]{1,2,0:T(8,128)(2,1)S(1)} %copy-done.1, f32[2048]{0:T(1024)S(1)} %copy-done.14), kind=kOutput, calls=%fused_computation.46 | convolution fusion | flops 6774128640 | bytes 58335232 | tf_op jit(solution)/shard_map/transpose(jvp())/dot_general | solution.py:26
  252.9 207.7 %shard_map.178 = (bf16[2,16,40,2560]{3,2,1,0:T(8,128)(2,1)}, bf16[2,16,40,2560]{3,2,1,0:T(8,128)(2,1)}, bf16[2,16,160,640]{3,2,1,0:T(8,128)(2,1)}, f32[2,40,2560...) custom-call(bf16[8,2,40,2560]{3,2,1,0:T(8,128)(2,1)} %bitcast.99, ...), custom_call_target="tpu_custom_call" | custom-call | tf_op jit(solution)/shard_map/pallas_call | solution.py:214
  460.7 6.8 %copy.31 = bf16[2,640,2560]{2,1,0:T(8,128)(2,1)} copy(bf16[2,640,2560]{2,1,0:T(8,128)(2,1)} %bitcast.84) | data formatting | bytes 13107200
  467.4 3.3 copy.32
  470.8 1.4 slice-done.1
  472.2 3.3 copy.33
  478.2 0.9 copy.37
  (60 shorter events, 5.2 us)
Async XLA Ops:
  3.6 38.2 %copy-start = (bf16[1,2048,640]{1,2,0:T(8,128)(2,1)}, bf16[1,2048,640]{1,2,0:T(8,128)(2,1)S(1)}, u32[]{:S(2)}) copy-start(bf16[1,2048,640]{1,2,0:T(8,128)(2,1)S(1)} %copy.20) | copy-start | bytes 7864324
  3.7 16.7 %slice-start.4 = ((s8[6553600]{0:T(1024)(128)(4,1)}), s8[4194304]{0:T(1024)(128)(4,1)S(1)}, s32[]{:S(2)}) async-start(s8[6553600]{0:T(1024)(128)(4,1)} %bitcast.89), calls=%async_computation.4 | async-start | bytes 8388608
  4.2 16.1 %copy-start.13 = (f32[2048]{0:T(1024)}, f32[2048]{0:T(1024)S(1)}, u32[]{:S(2)}) copy-start(f32[2048]{0:T(1024)S(1)} %add_rsqrt_fusion) | copy-start | bytes 24580
  4.2 16.1 %slice-start.5 = ((s8[6553600]{0:T(1024)(128)(4,1)}), s8[2359296]{0:T(1024)(128)(4,1)S(1)}, s32[]{:S(2)}) async-start(s8[6553600]{0:T(1024)(128)(4,1)} %bitcast.89), calls=%async_computation.5 | async-start | bytes 4718592
  52.8 11.9 %copy-start.3 = (bf16[2048,640]{0,1:T(8,128)(2,1)}, bf16[2048,640]{0,1:T(8,128)(2,1)S(1)}, u32[]{:S(2)}) copy-start(bf16[2048,640]{0,1:T(8,128)(2,1)S(1)} %get-tuple-element.30) | copy-start | bytes 7864324
  52.8 11.8 %copy-start.11 = (f32[2048]{0:T(1024)}, f32[2048]{0:T(1024)S(1)}, u32[]{:S(2)}) copy-start(f32[2048]{0:T(1024)S(1)} %get-tuple-element.29) | copy-start | bytes 24580
  52.8 11.8 %copy-start.4 = (bf16[1,2048,640]{2,1,0:T(8,128)(2,1)S(1)}, bf16[1,2048,640]{2,1,0:T(8,128)(2,1)}, u32[]{:S(2)}) copy-start(bf16[1,2048,640]{2,1,0:T(8,128)(2,1)} %param.12) | copy-start | bytes 7864324
  108.5 48.5 %slice-start.2 = ((s8[6553600]{0:T(1024)(128)(4,1)}), s8[2359296]{0:T(1024)(128)(4,1)S(1)}, s32[]{:S(2)}) async-start(s8[6553600]{0:T(1024)(128)(4,1)} %bitcast.86), calls=%async_computation.2 | async-start | bytes 4718592
  129.0 28.0 %slice-start.3 = ((s8[6553600]{0:T(1024)(128)(4,1)}), s8[4194304]{0:T(1024)(128)(4,1)S(1)}, s32[]{:S(2)}) async-start(s8[6553600]{0:T(1024)(128)(4,1)} %bitcast.86), calls=%async_computation.3 | async-start | bytes 8388608
  145.1 11.8 %copy-start.15 = (bf16[2048,2560]{1,0:T(8,128)(2,1)S(1)}, bf16[2048,2560]{1,0:T(8,128)(2,1)}, u32[]{:S(2)}) copy-start(bf16[2048,2560]{1,0:T(8,128)(2,1)} %get-tuple-element.31) | copy-start | bytes 31457284
  165.4 19.1 %copy-start.12 = (f32[2048]{0:T(1024)S(1)}, f32[2048]{0:T(1024)}, u32[]{:S(2)}) copy-start(f32[2048]{0:T(1024)} %copy-done.11) | copy-start | bytes 24580
  187.5 17.1 %slice-start.6 = ((s8[6553600]{0:T(1024)(128)(4,1)}), s8[4194304]{0:T(1024)(128)(4,1)S(1)}, s32[]{:S(2)}) async-start(s8[6553600]{0:T(1024)(128)(4,1)} %bitcast.92), calls=%async_computation.6 | async-start | bytes 8388608
  192.0 12.6 %slice-start.7 = ((s8[6553600]{0:T(1024)(128)(4,1)}), s8[2359296]{0:T(1024)(128)(4,1)S(1)}, s32[]{:S(2)}) async-start(s8[6553600]{0:T(1024)(128)(4,1)} %bitcast.92), calls=%async_computation.7 | async-start | bytes 4718592
  204.6 11.2 %copy-start.1 = (bf16[1,2048,640]{1,2,0:T(8,128)(2,1)S(1)}, bf16[1,2048,640]{1,2,0:T(8,128)(2,1)}, u32[]{:S(2)}) copy-start(bf16[1,2048,640]{1,2,0:T(8,128)(2,1)} %copy-done) | copy-start | bytes 7864324
  204.6 11.2 %copy-start.14 = (f32[2048]{0:T(1024)S(1)}, f32[2048]{0:T(1024)}, u32[]{:S(2)}) copy-start(f32[2048]{0:T(1024)} %copy-done.13) | copy-start | bytes 24580
  460.6 6.8 %copy-start.2 = (bf16[2,16,40,2560]{3,2,1,0:T(8,128)(2,1)S(1)}, bf16[2,16,40,2560]{3,2,1,0:T(8,128)(2,1)}, u32[]{:S(2)}) copy-start(bf16[2,16,40,2560]{3,2,1,0:T(8,128)(2,1)} %get-tuple-element.19) | copy-start | bytes 19660804
  460.7 10.1 %slice-start = ((s8[6553600]{0:T(1024)(128)(4,1)}), s8[4194304]{0:T(1024)(128)(4,1)S(1)}, s32[]{:S(2)}) async-start(s8[6553600]{0:T(1024)(128)(4,1)} %bitcast.80), calls=%async_computation | async-start | bytes 8388608
  467.4 4.7 slice-start.1
  472.2 3.3 copy-start.10
  472.2 4.2 copy-start.9
  472.2 5.1 %copy-start.8 = (f32[2,160,640]{2,1,0:T(8,128)S(1)}, f32[2,160,640]{2,1,0:T(8,128)}, u32[]{:S(2)}) copy-start(f32[2,160,640]{2,1,0:T(8,128)} %get-tuple-element.49) | copy-start | bytes 2457604
  472.2 6.0 %copy-start.7 = (f32[2,40,2560]{2,1,0:T(8,128)S(1)}, f32[2,40,2560]{2,1,0:T(8,128)}, u32[]{:S(2)}) copy-start(f32[2,40,2560]{2,1,0:T(8,128)} %get-tuple-element.50) | copy-start | bytes 2457604
  475.5 3.6 copy-start.6
  475.5 4.5 copy-start.5

commit v2 on v1

v2 whole, which is shorter than its diff:
```python
import functools

import jax
import jax.numpy as jnp
from jax import lax
from jax.experimental import pallas as pl
from jax.experimental.pallas import tpu as pltpu
from jax.sharding import PartitionSpec as P

F32, BF16 = jnp.float32, jnp.bfloat16
MESH = pl.DeviceIdType.MESH

T, D, FF = 2048, 640, 2560
F = 256
TILES = FF // F
R = 512
STEPS = T // R
HOPS = 7
L0 = TILES + 2
LAST = L0 + TILES


def ring(p):
    return p + (p // 4) * (11 - 2 * p)


def dot(a, b):
    return jnp.dot(a, b, preferred_element_type=F32)


def dot_nt(a, b):
    return lax.dot_general(a, b, (((1,), (1,)), ((), ())), preferred_element_type=F32)


def dot_tn(a, b):
    return lax.dot_general(a, b, (((0,), (0,)), ((), ())), preferred_element_type=F32)


def scale_of(wide):
    return lax.rsqrt(jnp.mean(wide * wide, -1, keepdims=True) + 1e-6)


def where_am_i():
    rep, dp = lax.axis_index("rep"), lax.axis_index("dp")
    chip, core = dp // 2, dp % 2
    way = 1 - 2 * core
    return rep, dp, chip, core, way, ring(chip)


def remote(src, dst, send, recv, rep, device):
    return pltpu.make_async_remote_copy(
        src_ref=src, dst_ref=dst, send_sem=send, recv_sem=recv, device_id=(rep, device), device_id_type=MESH)


def grad_kernel(x_hbm, dy_hbm, wg_hbm, wu_hbm, wd_hbm,
                gg_hbm, gd_hbm, gu_hbm, hid_hbm,
                h, a, a0t, a1t, dy, acc, hid, dg, du, wg, wu, wd, gu,
                own, other, hop, ownd, otherd, hopd, gg, gd,
                io_sem, w_sem, gu_sem, hid_sem,
                half_send, half_recv, hop_send, hop_recv, dhalf_send, dhalf_recv, dhop_send, dhop_recv):
    rep, dp, chip, core, way, place = where_am_i()
    to = 2 * ring((place + way + 8) % 8) + core
    back = 2 * ring((place - way + 8) % 8) + core
    partner = dp + way

    barrier = pltpu.get_barrier_semaphore()
    for device in (to, back, partner):
        pl.semaphore_signal(barrier, inc=1, device_id=(rep, device), device_id_type=MESH)

    x_copy = pltpu.make_async_copy(x_hbm, h, io_sem.at[0])
    dy_copy = pltpu.make_async_copy(dy_hbm, dy, io_sem.at[1])
    x_copy.start()

    def cols(j):
        return pl.ds(pl.multiple_of(j * F, F), F)

    def rows(t):
        return pl.ds(pl.multiple_of(t * R, R), R)

    def w_copies(k):
        layer, j, slot = (k // TILES) % 2, k % TILES, k % 2
        return (
            pltpu.make_async_copy(wg_hbm.at[layer, :, cols(j)], wg.at[slot], w_sem.at[0, slot]),
            pltpu.make_async_copy(wu_hbm.at[layer, :, cols(j)], wu.at[slot], w_sem.at[1, slot]),
            pltpu.make_async_copy(wd_hbm.at[layer, cols(j), :], wd.at[slot], w_sem.at[2, slot]),
        )

    def w_start(k):
        for c in w_copies(k):
            c.start()

    def w_wait(k):
        for c in w_copies(k):
            c.wait()

    def gu_copies(k, out):
        j, t, slot = k // STEPS, k % STEPS, k % 2
        for n in range(2):
            there, here = gu_hbm.at[n, j, rows(t), :], gu.at[slot, n]
            yield pltpu.make_async_copy(here, there, gu_sem.at[n, slot]) if out else pltpu.make_async_copy(
                there, here, gu_sem.at[n, slot])

    def hid_copy(j, out):
        there, here = hid_hbm.at[j], hid.at[j % 2]
        return (pltpu.make_async_copy(here, there, hid_sem.at[j % 2]) if out
                else pltpu.make_async_copy(there, here, hid_sem.at[j % 2]))

    w_start(0)
    x_copy.wait()
    dy_copy.start()

    def owner(s):
        return ring((place - way * (1 + s) + 16) % 8)

    def half(i):
        return remote(own.at[i % TILES, :, 1 - core], other.at[i], half_send.at[i], half_recv.at[i], rep, partner)

    def hop_copy(i, s, src):
        return remote(src, hop.at[i, s], hop_send.at[i, s], hop_recv.at[i, s], rep, to)

    def added(i, who):
        return own.at[i % TILES, who, core][...].astype(F32) + other.at[i, who][...].astype(F32)

    def half_d(d, q):
        rows_ = pl.ds(pl.multiple_of((2 * q + 1 - core) * 160, 32), 160)
        return remote(ownd.at[d, rows_], otherd.at[d, q], dhalf_send.at[d, q], dhalf_recv.at[d, q], rep, partner)

    def hop_copy_d(d, s, src):
        return remote(src, hopd.at[d, s], dhop_send.at[d, s], dhop_recv.at[d, s], rep, to)

    def rows_d(who):
        return pl.ds(pl.multiple_of((2 * who + core) * 160, 32), 160)

    def added_d(d, who):
        return ownd.at[d, rows_d(who)][...].astype(F32) + otherd.at[d, who][...].astype(F32)

    def serve(n):
        for age in range(1, HOPS + 2):
            c = n - age
            late = jnp.where(c >= L0, 1, 0)
            i = c - 2 * late

            @pl.when(((c >= 0) & (c < TILES)) | ((c >= L0) & (c < LAST)))
            def _():
                s = age - 1
                if s == 0:
                    half(i).wait_recv()
                    mine = own.at[i % TILES, owner(0), core]
                    mine[...] = added(i, owner(0)).astype(BF16)
                    hop_copy(i, 0, mine).start()
                else:
                    slot = hop.at[i, s - 1]
                    hop_copy(i, s - 1, slot).wait_recv()
                    who = owner(s)
                    new = (slot[...].astype(F32) + added(i, who)).astype(BF16)
                    if s < HOPS:
                        slot[...] = new
                        hop_copy(i, s, slot).start()
                    else:
                        gg.at[1 - late][:, :, cols(i % TILES)] = new
                        half(i).wait_send()
                        for r in range(HOPS):
                            hop_copy(i, r, slot).wait_send()

    def serve_d(d, age):
        s = age - 1

        @pl.when(s == 0)
        def _():
            for q in range(8):
                half_d(d, q).wait_recv()
            mine = ownd.at[d, rows_d(owner(0))]
            mine[...] = added_d(d, owner(0)).astype(BF16)
            hop_copy_d(d, 0, mine).start()

        @pl.when((s > 0) & (s <= HOPS))
        def _():
            slot = hopd.at[d, s - 1]
            hop_copy_d(d, s - 1, slot).wait_recv()
            new = (slot[...].astype(F32) + added_d(d, owner(s))).astype(BF16)

            @pl.when(s < HOPS)
            def _():
                slot[...] = new
                hop_copy_d(d, s, slot).start()

            @pl.when(s == HOPS)
            def _():
                gd.at[d][...] = new
                for q in range(8):
                    half_d(d, q).wait_send()
                for r in range(HOPS):
                    hop_copy_d(d, r, slot).wait_send()

    def put(i, n, t_, grad):
        g = dot(t_[...], grad[...]).astype(BF16)
        for o in range(16):
            own.at[i % TILES, o // 2, o % 2, n][...] = g[40 * o : 40 * o + 40]

    def norm(t, to_t):
        wide = h[rows(t), :].astype(F32)
        one = (wide * scale_of(wide)).astype(BF16)
        a[rows(t), :] = one
        to_t[:, rows(t)] = one.T
        acc[rows(t), :] = jnp.zeros((R, D), F32)

    def first(t, z):
        norm(t, a0t)
        return z

    lax.fori_loop(0, STEPS, first, 0)

    def forward(j, z):
        slot = j % 2
        w_wait(j)
        w_start(j + 1)

        @pl.when(j >= 2)
        def _():
            hid_copy(j - 2, True).wait()

        def step(t, z):
            k = j * STEPS + t
            gate, up = dot(a[rows(t), :], wg[slot]), dot(a[rows(t), :], wu[slot])

            @pl.when(k >= 2)
            def _():
                for c in gu_copies(k - 2, True):
                    c.wait()

            gu.at[t % 2, 0][...] = gate
            gu.at[t % 2, 1][...] = up
            for c in gu_copies(k, True):
                c.start()
            hidden = (gate * jax.nn.sigmoid(gate) * up).astype(BF16)
            hid.at[slot][rows(t), :] = hidden
            acc[rows(t), :] += dot(hidden, wd[slot])
            return z

        lax.fori_loop(0, STEPS, step, 0)
        hid_copy(j, True).start()
        return z

    lax.fori_loop(0, TILES, forward, 0)
    for k in (TILES * STEPS - 2, TILES * STEPS - 1):
        for c in gu_copies(k, True):
            c.wait()
    for j in (TILES - 2, TILES - 1):
        hid_copy(j, True).wait()

    def second(t, z):
        h[rows(t), :] = (h[rows(t), :].astype(F32) + acc[rows(t), :].astype(BF16).astype(F32)).astype(BF16)
        norm(t, a1t)
        return z

    lax.fori_loop(0, STEPS, second, 0)
    dy_copy.wait()
    pl.semaphore_wait(barrier, 3)

    def back_of(gate, up, by_hidden, slot, t):
        sig = jax.nn.sigmoid(gate)
        silu = gate * sig
        dg[rows(t), :] = (by_hidden * up * (sig + silu * (1.0 - sig))).astype(BF16)
        du[rows(t), :] = (by_hidden * silu).astype(BF16)
        return silu

    def tile(j, z):
        k = TILES + j
        slot = k % 2
        w_wait(k)
        w_start(k + 1)

        def step(t, z):
            gate, up = dot(a[rows(t), :], wg[slot]), dot(a[rows(t), :], wu[slot])
            by_hidden = dot_nt(dy[rows(t), :], wd[slot]).astype(BF16).astype(F32)
            silu = back_of(gate, up, by_hidden, slot, t)
            hid.at[0][rows(t), :] = (silu * up).astype(BF16)
            return z

        lax.fori_loop(0, STEPS, step, 0)
        serve(j)
        put(j, 0, a1t, dg)
        put(j, 1, a1t, du)
        half(j).start()
        ownd.at[1][cols(j), :] = dot_tn(hid[0], dy[...]).astype(BF16)

        def step_a(t, z):
            acc[rows(t), :] += dot_nt(dg[rows(t), :], wg[slot]) + dot_nt(du[rows(t), :], wu[slot])
            return z

        @pl.when(j == 0)
        def _():
            def clear(t, z):
                acc[rows(t), :] = jnp.zeros((R, D), F32)
                return z
            lax.fori_loop(0, STEPS, clear, 0)

        lax.fori_loop(0, STEPS, step_a, 0)
        return z

    lax.fori_loop(0, TILES, tile, 0)
    for q in range(8):
        half_d(1, q).start()
    hid_copy(0, False).start()

    def by_h(t, z):
        by_a = acc[rows(t), :].astype(BF16).astype(F32)
        wide = h[rows(t), :].astype(F32)
        scale = scale_of(wide)
        by_wide = scale * by_a - wide * (scale * scale * scale * jnp.mean(by_a * wide, -1, keepdims=True))
        dy[rows(t), :] = (dy[rows(t), :].astype(F32) + by_wide.astype(BF16).astype(F32)).astype(BF16)
        return z

    lax.fori_loop(0, STEPS, by_h, 0)

    def down(r, z):
        def one(jj, z):
            j = r * (TILES // 2) + jj
            hid_copy(j, False).wait()

            @pl.when(j + 1 < TILES)
            def _():
                hid_copy(j + 1, False).start()

            ownd.at[0][cols(j), :] = dot_tn(hid[j % 2], dy[...]).astype(BF16)
            return z

        lax.fori_loop(0, TILES // 2, one, 0)
        serve(TILES + r)
        serve_d(1, 1 + r)
        return z

    for c in gu_copies(0, False):
        c.start()
    lax.fori_loop(0, 2, down, 0)
    for q in range(8):
        half_d(0, q).start()

    def tile0(j, z):
        k = 2 * TILES + j
        slot = k % 2
        w_wait(k)

        @pl.when(j + 1 < TILES)
        def _():
            w_start(k + 1)

        def step(t, z):
            n = j * STEPS + t
            by_hidden = dot_nt(dy[rows(t), :], wd[slot]).astype(BF16).astype(F32)
            for c in gu_copies(n, False):
                c.wait()

            @pl.when(n + 1 < TILES * STEPS)
            def _():
                for c in gu_copies(n + 1, False):
                    c.start()

            back_of(gu[t % 2, 0], gu[t % 2, 1], by_hidden, slot, t)
            return z

        lax.fori_loop(0, STEPS, step, 0)
        serve(L0 + j)
        serve_d(1, 3 + j)
        serve_d(0, 1 + j)
        put(TILES + j, 0, a0t, dg)
        put(TILES + j, 1, a0t, du)
        half(TILES + j).start()
        return z

    lax.fori_loop(0, TILES, tile0, 0)

    def drain(r, z):
        serve(LAST + r)
        return z

    lax.fori_loop(0, HOPS + 1, drain, 0)
    out = [pltpu.make_async_copy(gg, gg_hbm, io_sem.at[0]), pltpu.make_async_copy(gd, gd_hbm, io_sem.at[1])]
    for c in out:
        c.start()
    for c in out:
        c.wait()


def grads(x, dy, wg, wu, wd):
    any_ = pl.BlockSpec(memory_space=pl.ANY)
    dma, vmem = pltpu.SemaphoreType.DMA, pltpu.VMEM
    s = jax.ShapeDtypeStruct
    block = (2, 40, F)
    out = pl.pallas_call(
        grad_kernel,
        out_shape=[s((2, 2, 40, FF), BF16), s((2, 160, D), BF16),
                   s((2, TILES, T, F), F32), s((TILES, T, F), BF16)],
        in_specs=[any_] * 5,
        out_specs=[any_] * 4,
        scratch_shapes=[
            vmem((T, D), BF16), vmem((T, D), BF16), vmem((D, T), BF16), vmem((D, T), BF16), vmem((T, D), BF16),
            vmem((T, D), F32), vmem((2, T, F), BF16), vmem((T, F), BF16), vmem((T, F), BF16),
            vmem((2, D, F), BF16), vmem((2, D, F), BF16), vmem((2, F, D), BF16), vmem((2, 2, R, F), F32),
            vmem((TILES, 8, 2, *block), BF16), vmem((2 * TILES, 8, *block), BF16), vmem((2 * TILES, HOPS, *block), BF16),
            vmem((2, FF, D), BF16), vmem((2, 8, 160, D), BF16), vmem((2, HOPS, 160, D), BF16),
            vmem((2, 2, 40, FF), BF16), vmem((2, 160, D), BF16),
            dma((2,)), dma((3, 2)), dma((2, 2)), dma((2,)),
            dma((2 * TILES,)), dma((2 * TILES,)), dma((2 * TILES, HOPS)), dma((2 * TILES, HOPS)),
            dma((2, 8)), dma((2, 8)), dma((2, HOPS)), dma((2, HOPS)),
        ],
        compiler_params=pltpu.CompilerParams(
            collective_id=1, has_side_effects=True, vmem_limit_bytes=67043328),
    )(x, dy, wg, wu, wd)
    return out[:2]


def update_kernel(count, *refs):
    gg_hbm, gd_hbm, w, m, v = refs[0], refs[1], refs[2:5], refs[5:8], refs[8:11]
    w_out, m_out, v_out = refs[11:14], refs[14:17], refs[17:20]
    (gg, gd, mg, md, vg, vd, wg, wd, sums, g_sem, load_sem, sum_send, sum_recv,
     ag_send, ag_recv, d2d_send, d2d_recv, store_sem) = refs[20:]
    items = [(0, 0), (1, 0), (2, 0), (0, 1), (1, 1), (2, 1)]

    def at(k, big, small):
        which, layer_ = items[k]
        return small.at[layer_] if which == 2 else big.at[layer_, which]

    rep, dp, chip, core, way, place = where_am_i()
    to = 2 * ring((place + way + 8) % 8) + core
    partner = dp + way

    barrier = pltpu.get_barrier_semaphore()
    for off in range(1, 16):
        pl.semaphore_signal(barrier, inc=1, device_id=(rep, (dp + off) % 16), device_id_type=MESH)

    g_loads = [pltpu.make_async_copy(gg_hbm, gg, g_sem.at[0]), pltpu.make_async_copy(gd_hbm, gd, g_sem.at[1])]
    for c in g_loads:
        c.start()
    loads = []
    for k, (which, layer_) in enumerate(items):
        for n, (src, dst) in enumerate((
            (m[which].at[layer_], at(k, mg, md)),
            (v[which].at[layer_], at(k, vg, vd)),
            (w[which].at[layer_, dp], at(k, wg, wd)),
        )):
            c = pltpu.make_async_copy(src, dst, load_sem.at[k, n])
            c.start()
            loads.append(c)
    for c in g_loads:
        c.wait()

    squares = jnp.zeros((8, 128), F32)
    for k in range(6):
        g = at(k, gg, gd)[...].astype(F32)
        g = g * g
        part = g[0:8]
        for i in range(1, g.shape[0] // 8):
            part = part + g[8 * i : 8 * i + 8]
        for i in range(part.shape[1] // 128):
            squares = squares + part[:, 128 * i : 128 * i + 128]
    sums.at[dp][...] = squares
    pl.semaphore_wait(barrier, 15)

    def sum_copy(off):
        return remote(sums.at[dp], sums.at[dp], sum_send.at[off], sum_recv.at[off], rep, (dp + off) % 16)

    for off in range(1, 16):
        sum_copy(off).start()
    for c in loads:
        c.wait()
    for off in range(1, 16):
        sum_copy(off).wait_recv()
    mean = jnp.sum(sums[...]) / count
    factor = jnp.minimum(1.0, 0.5 * lax.rsqrt(jnp.full((8, 128), mean + 1e-30, F32)))[0:1, 0:1]

    def block(k, who):
        which, layer_ = items[k]
        return w_out[which].at[layer_, who]

    def gather_copy(k, s, who, src=None):
        src = block(k, who) if src is None else src
        return remote(src, block(k, who), ag_send.at[k, s], ag_recv.at[k, s], rep, to)

    def d2d_copy(k, s, who, src=None):
        src = block(k, who) if src is None else src
        return remote(src, block(k, who), d2d_send.at[k, s], d2d_recv.at[k, s], rep, partner)

    stores = []
    for k, (which, layer_) in enumerate(items):
        g = at(k, gg, gd)[...].astype(F32) * factor
        mk, vk, wk = at(k, mg, md), at(k, vg, vd), at(k, wg, wd)
        new_m = 0.9 * mk[...] + 0.1 * g
        new_v = 0.95 * vk[...] + 0.05 * g * g
        wide = wk[...].astype(F32)
        wk[...] = (wide - 0.02 * (new_m * lax.rsqrt(new_v + 1e-8) + 0.1 * wide)).astype(BF16)
        mk[...] = new_m
        vk[...] = new_v
        gather_copy(k, 0, dp, wk).start()
        d2d_copy(k, 0, dp, wk).start()
        for n, (src, dst) in enumerate((
            (wk, block(k, dp)), (mk, m_out[which].at[layer_]), (vk, v_out[which].at[layer_]))):
            c = pltpu.make_async_copy(src, dst, store_sem.at[k, n])
            c.start()
            stores.append(c)

    def source(s):
        return 2 * ring((place - way * (1 + s) + 16) % 8) + core

    def gather(s, z):
        for k in range(6):
            who = source(s)
            gather_copy(k, s, who).wait_recv()
            gather_copy(k, s + 1, who).start()
            d2d_copy(k, s + 1, who).start()
        return z

    lax.fori_loop(0, 6, gather, 0)
    for k in range(6):
        who = source(6)
        gather_copy(k, 6, who).wait_recv()
        d2d_copy(k, 7, who).start()

    for c in stores:
        c.wait()
    for off in range(1, 16):
        sum_copy(off).wait_send()

    def drain(s, z):
        for k in range(6):
            gather_copy(k, s, dp).wait_send()
            d2d_copy(k, s, dp).wait_send()
            d2d_copy(k, s, dp).wait_recv()
        return z

    lax.fori_loop(0, 7, drain, 0)
    for k in range(6):
        d2d_copy(k, 7, dp).wait_send()
        d2d_copy(k, 7, dp).wait_recv()


def update(count, gg, gd, weights, m, v):
    G, S = (2, 2, 40, FF), (2, 160, D)
    any_ = pl.BlockSpec(memory_space=pl.ANY)
    dma, vmem = pltpu.SemaphoreType.DMA, pltpu.VMEM
    return pl.pallas_call(
        functools.partial(update_kernel, count),
        out_shape=[
            *(jax.ShapeDtypeStruct(t.shape, BF16) for t in weights),
            *(jax.ShapeDtypeStruct(t.shape, F32) for t in (*m, *v)),
        ],
        in_specs=[any_] * 11,
        out_specs=[any_] * 9,
        scratch_shapes=[
            vmem(G, BF16), vmem(S, BF16), vmem(G, F32), vmem(S, F32), vmem(G, F32), vmem(S, F32), vmem(G, BF16), vmem(S, BF16),
            vmem((16, 8, 128), F32),
            dma((2,)), dma((6, 3)), dma((16,)), dma((16,)),
            dma((6, 7)), dma((6, 7)), dma((6, 8)), dma((6, 8)), dma((6, 3)),
        ],
        compiler_params=pltpu.CompilerParams(
            collective_id=0, has_side_effects=True, vmem_limit_bytes=24 * 1024 * 1024),
    )(gg, gd, *weights, *m, *v)


def solution(mesh):
    def body(x, dy, *arrays):
        weights, m, v = (arrays[i : i + 3] for i in (0, 3, 6))
        gg, gd = grads(x[0], dy[0], *weights)
        blocks = [w.reshape(2, 16, -1, w.shape[-1]) for w in weights]
        count = float(sum(w.size for w in weights))
        out = update(count, gg, gd, blocks, m, v)
        return (*(o.reshape(w.shape) for o, w in zip(out[:3], weights)), *out[3:])

    whole, rows = P(None, None, None), P(None, "dp", None)
    return jax.shard_map(
        body,
        mesh=mesh,
        in_specs=(P(("rep", "dp"), None, None),) * 2 + (whole,) * 3 + (rows,) * 6,
        out_specs=(P("rep", None, None),) * 3 + (P("rep", "dp", None),) * 6,
        check_vma=False,
    )
```

time: 490 us -> 395 us (0.81); the launches traced: 481 us -> 393 us
  matrix products: 241 us -> 0 us
  Pallas kernels: 208 us -> 360 us
  local copies, waits for them, and re-layouts: 26.3 us -> 32.6 us
  other arithmetic: 5.05 us -> 0 us
    dot_general x15 -> x0, matrix products: 241 us -> none  [the longest x5 89.2 us: layer(): gate = jnp.dot(a, wg, preferred_element_type=F32)]
    pallas_call x1 -> x2, Pallas kernels: 208 us -> 360 us  [the longest x1 255 us: grads(): pl.pallas_call(grad_kernel, out_shape=[s((2, 2, 40, FF), BF16), s((2, 160...]
    unnamed x59 -> x35, local copies, waits for them, and re-layouts: 26.3 us -> 32.6 us
where the time goes in v2:
time: 395 us; the launch traced here: 393 us
  Pallas kernels  360 us (91%)
  local copies, waits for them, and re-layouts  32.6 us (8%)
    pallas_call x1, Pallas kernels, grads(): pl.pallas_call(grad_kernel, out_shape=[s((2, 2, 40, FF), BF16), s((2, 160...  255 us
    pallas_call x1, Pallas kernels, update(): pl.pallas_call(functools.partial(update_kernel, count), out_shape=[*(jax....  105 us
    unnamed x35, local copies, waits for them, and re-layouts  32.6 us

profile of v2, /device:TPU:0, one launch (start us, length us, event | category | flops | bytes accessed | tf_op | source)
XLA Modules:
  0.0 393.2 jit_solution(15553615513422815496)
XLA Ops:
  0.6 254.9 %shard_map.178 = (bf16[2,2,40,2560]{3,2,1,0:T(8,128)(2,1)}, bf16[2,160,640]{2,1,0:T(8,128)(2,1)}, f32[2,10,2048,256]{3,2,1,0:T(8,128)}, bf16[10,2048,256]{2,1,0:T(8,128)(2,1)}) custom-call(bf16[2048,640]{1,0:T(8,128)(2,1)} %bitcast.14, bf16[2048,640]{1,0:T(8,128)(2,1)} %bitcast.15, bf16[2,640,2560]{2,1,0:T(8,128)(2,1)} %wg_hbm.1, ...), custom_call_target="tpu_custom_call" | custom-call | tf_op jit(solution)/shard_map/pallas_call | solution.py:390
  255.6 0.0 copy-start.5
  255.6 1.1 copy-done.5
  256.7 1.1 copy-done.6
  257.9 1.1 copy-done.7
  259.0 1.1 copy-done.8
  260.2 1.1 copy-done.9
  261.3 1.1 copy-done.10
  262.4 1.1 copy-done.11
  263.6 1.0 copy-done.12
  264.6 105.0 %shard_map.179 = (bf16[2,16,40,2560]{3,2,1,0:T(8,128)(2,1)S(1)}, bf16[2,16,40,2560]{3,2,1,0:T(8,128)(2,1)S(1)}, bf16[2,16,160,640]{3,2,1,0:T(8,128)(2,1)S(1)}, f...) custom-call(bf16[2,2,40,2560]{3,2,1,0:T(8,128)(2,1)S(1)} %copy-done., ...), custom_call_target="tpu_custom_call" | custom-call | tf_op jit(solution)/shard_map/pallas_call | solution.py:541
  369.6 0.0 copy-start
  369.6 2.8 copy-done
  372.4 0.9 copy-done.3
  373.3 2.8 copy-done.2
  376.0 6.2 %copy.29 = bf16[2,640,2560]{2,1,0:T(8,128)(2,1)} copy(bf16[2,640,2560]{2,1,0:T(8,128)(2,1)} %bitcast.10) | data formatting | bytes 13107200
  382.3 2.8 copy.30
  385.1 2.8 copy.31
  387.9 0.9 copy.32
  388.8 0.9 copy.33
  389.7 0.9 copy.34
  390.5 0.9 copy.35
  391.4 0.9 copy.36
  392.3 0.9 copy.37
  (13 shorter events, 0.0 us)
Async XLA Ops:
  255.6 1.1 copy-start.5
  256.7 1.1 copy-start.6
  257.9 1.1 copy-start.7
  259.0 1.1 copy-start.8
  260.2 1.1 copy-start.9
  261.3 1.1 copy-start.10
  262.4 1.1 copy-start.11
  263.6 1.0 copy-start.12
  369.6 2.8 copy-start
  372.4 0.9 copy-start.3
  373.3 2.8 copy-start.2
  376.0 6.2 %copy-start.1 = (bf16[2,16,40,2560]{3,2,1,0:T(8,128)(2,1)S(1)}, bf16[2,16,40,2560]{3,2,1,0:T(8,128)(2,1)}, u32[]{:S(2)}) copy-start(bf16[2,16,40,2560]{3,2,1,0:T(8,128)(2,1)} %copy-done) | copy-start | bytes 19660804
  385.1 2.8 copy-start.4

commit v3 on v2

--- a/solution.py
+++ b/solution.py
@@ -15,6 +15,7 @@
 TILES = FF // F
 R = 512
 STEPS = T // R
+DEPTH = 4
 HOPS = 7
 L0 = TILES + 2
 LAST = L0 + TILES
@@ -34,6 +35,10 @@
 
 def dot_tn(a, b):
     return lax.dot_general(a, b, (((0,), (0,)), ((), ())), preferred_element_type=F32)
+
+
+def sigmoid(x):
+    return jax.nn.sigmoid(x)
 
 
 def scale_of(wide):
@@ -75,7 +80,7 @@
         return pl.ds(pl.multiple_of(j * F, F), F)
 
     def rows(t):
-        return pl.ds(pl.multiple_of(t * R, R), R)
+        return pl.ds(t * R, R) if isinstance(t, int) else pl.ds(pl.multiple_of(t * R, R), R)
 
     def w_copies(k):
         layer, j, slot = (k // TILES) % 2, k % TILES, k % 2
@@ -94,16 +99,16 @@
             c.wait()
 
     def gu_copies(k, out):
-        j, t, slot = k // STEPS, k % STEPS, k % 2
+        j, t, slot = k // STEPS, k % STEPS, k % DEPTH
         for n in range(2):
             there, here = gu_hbm.at[n, j, rows(t), :], gu.at[slot, n]
             yield pltpu.make_async_copy(here, there, gu_sem.at[n, slot]) if out else pltpu.make_async_copy(
                 there, here, gu_sem.at[n, slot])
 
     def hid_copy(j, out):
-        there, here = hid_hbm.at[j], hid.at[j % 2]
-        return (pltpu.make_async_copy(here, there, hid_sem.at[j % 2]) if out
-                else pltpu.make_async_copy(there, here, hid_sem.at[j % 2]))
+        there, here = hid_hbm.at[j], hid.at[j % 3]
+        return (pltpu.make_async_copy(here, there, hid_sem.at[j % 3]) if out
+                else pltpu.make_async_copy(there, here, hid_sem.at[j % 3]))
 
     w_start(0)
     x_copy.wait()
@@ -210,42 +215,47 @@
 
     lax.fori_loop(0, STEPS, first, 0)
 
+    hid.at[2][rows(STEPS - 1), :] = jnp.zeros((R, F), BF16)
+    wd.at[1][...] = jnp.zeros((F, D), BF16)
+
     def forward(j, z):
-        slot = j % 2
         w_wait(j)
-        w_start(j + 1)
-
-        @pl.when(j >= 2)
+
+        @pl.when(j >= 3)
         def _():
-            hid_copy(j - 2, True).wait()
-
-        def step(t, z):
+            hid_copy(j - 3, True).wait()
+
+        def step(t, before):
             k = j * STEPS + t
-            gate, up = dot(a[rows(t), :], wg[slot]), dot(a[rows(t), :], wu[slot])
-
-            @pl.when(k >= 2)
+            h_slot, w_slot, t_before = before
+            acc[rows(t_before), :] += dot(hid[h_slot, rows(t_before), :], wd[w_slot])
+            gate, up = dot(a[rows(t), :], wg[j % 2]), dot(a[rows(t), :], wu[j % 2])
+            hidden = (gate * sigmoid(gate) * up).astype(BF16)
+
+            @pl.when(k >= DEPTH)
             def _():
-                for c in gu_copies(k - 2, True):
+                for c in gu_copies(k - DEPTH, True):
                     c.wait()
 
-            gu.at[t % 2, 0][...] = gate
-            gu.at[t % 2, 1][...] = up
+            gu.at[k % DEPTH, 0][...] = gate
+            gu.at[k % DEPTH, 1][...] = up
+            hid.at[j % 3][rows(t), :] = hidden
             for c in gu_copies(k, True):
                 c.start()
-            hidden = (gate * jax.nn.sigmoid(gate) * up).astype(BF16)
-            hid.at[slot][rows(t), :] = hidden
-            acc[rows(t), :] += dot(hidden, wd[slot])
-            return z
-
-        lax.fori_loop(0, STEPS, step, 0)
+
+        step(0, ((j + 2) % 3, (j + 1) % 2, STEPS - 1))
+        w_start(j + 1)
+        for t in range(1, STEPS):
+            step(t, (j % 3, j % 2, t - 1))
         hid_copy(j, True).start()
         return z
 
     lax.fori_loop(0, TILES, forward, 0)
-    for k in (TILES * STEPS - 2, TILES * STEPS - 1):
+    acc[rows(STEPS - 1), :] += dot(hid[(TILES - 1) % 3, rows(STEPS - 1), :], wd[(TILES - 1) % 2])
+    for k in range(TILES * STEPS - DEPTH, TILES * STEPS):
         for c in gu_copies(k, True):
             c.wait()
-    for j in (TILES - 2, TILES - 1):
+    for j in range(TILES - 3, TILES):
         hid_copy(j, True).wait()
 
     def second(t, z):
@@ -258,7 +268,7 @@
     pl.semaphore_wait(barrier, 3)
 
     def back_of(gate, up, by_hidden, slot, t):
-        sig = jax.nn.sigmoid(gate)
+        sig = sigmoid(gate)
         silu = gate * sig
         dg[rows(t), :] = (by_hidden * up * (sig + silu * (1.0 - sig))).astype(BF16)
         du[rows(t), :] = (by_hidden * silu).astype(BF16)
@@ -277,7 +287,8 @@
             hid.at[0][rows(t), :] = (silu * up).astype(BF16)
             return z
 
-        lax.fori_loop(0, STEPS, step, 0)
+        for t in range(STEPS):
+            step(t, 0)
         serve(j)
         put(j, 0, a1t, dg)
         put(j, 1, a1t, du)
@@ -302,6 +313,10 @@
     for q in range(8):
         half_d(1, q).start()
     hid_copy(0, False).start()
+    hid_copy(1, False).start()
+    for k in range(DEPTH - 1):
+        for c in gu_copies(k, False):
+            c.start()
 
     def by_h(t, z):
         by_a = acc[rows(t), :].astype(BF16).astype(F32)
@@ -318,11 +333,11 @@
             j = r * (TILES // 2) + jj
             hid_copy(j, False).wait()
 
-            @pl.when(j + 1 < TILES)
+            @pl.when(j + 2 < TILES)
             def _():
-                hid_copy(j + 1, False).start()
-
-            ownd.at[0][cols(j), :] = dot_tn(hid[j % 2], dy[...]).astype(BF16)
+                hid_copy(j + 2, False).start()
+
+            ownd.at[0][cols(j), :] = dot_tn(hid[j % 3], dy[...]).astype(BF16)
             return z
 
         lax.fori_loop(0, TILES // 2, one, 0)
@@ -330,8 +345,6 @@
         serve_d(1, 1 + r)
         return z
 
-    for c in gu_copies(0, False):
-        c.start()
     lax.fori_loop(0, 2, down, 0)
     for q in range(8):
         half_d(0, q).start()
@@ -351,12 +364,12 @@
             for c in gu_copies(n, False):
                 c.wait()
 
-            @pl.when(n + 1 < TILES * STEPS)
+            @pl.when(n + DEPTH - 1 < TILES * STEPS)
             def _():
-                for c in gu_copies(n + 1, False):
+                for c in gu_copies(n + DEPTH - 1, False):
                     c.start()
 
-            back_of(gu[t % 2, 0], gu[t % 2, 1], by_hidden, slot, t)
+            back_of(gu[n % DEPTH, 0], gu[n % DEPTH, 1], by_hidden, slot, t)
             return z
 
         lax.fori_loop(0, STEPS, step, 0)
@@ -395,12 +408,12 @@
         out_specs=[any_] * 4,
         scratch_shapes=[
             vmem((T, D), BF16), vmem((T, D), BF16), vmem((D, T), BF16), vmem((D, T), BF16), vmem((T, D), BF16),
-            vmem((T, D), F32), vmem((2, T, F), BF16), vmem((T, F), BF16), vmem((T, F), BF16),
-            vmem((2, D, F), BF16), vmem((2, D, F), BF16), vmem((2, F, D), BF16), vmem((2, 2, R, F), F32),
+            vmem((T, D), F32), vmem((3, T, F), BF16), vmem((T, F), BF16), vmem((T, F), BF16),
+            vmem((2, D, F), BF16), vmem((2, D, F), BF16), vmem((2, F, D), BF16), vmem((DEPTH, 2, R, F), F32),
             vmem((TILES, 8, 2, *block), BF16), vmem((2 * TILES, 8, *block), BF16), vmem((2 * TILES, HOPS, *block), BF16),
             vmem((2, FF, D), BF16), vmem((2, 8, 160, D), BF16), vmem((2, HOPS, 160, D), BF16),
             vmem((2, 2, 40, FF), BF16), vmem((2, 160, D), BF16),
-            dma((2,)), dma((3, 2)), dma((2, 2)), dma((2,)),
+            dma((2,)), dma((3, 2)), dma((2, DEPTH)), dma((3,)),
             dma((2 * TILES,)), dma((2 * TILES,)), dma((2 * TILES, HOPS)), dma((2 * TILES, HOPS)),
             dma((2, 8)), dma((2, 8)), dma((2, HOPS)), dma((2, HOPS)),
         ],
@@ -544,7 +557,7 @@
             *(jax.ShapeDtypeStruct(t.shape, BF16) for t in weights),
             *(jax.ShapeDtypeStruct(t.shape, F32) for t in (*m, *v)),
         ],
-        in_specs=[any_] * 11,
+        in_specs=[pl.BlockSpec(memory_space=pltpu.HBM)] * 11,
         out_specs=[any_] * 9,
         scratch_shapes=[
             vmem(G, BF16), vmem(S, BF16), vmem(G, F32), vmem(S, F32), vmem(G, F32), vmem(S, F32), vmem(G, BF16), vmem(S, BF16),
@@ -553,8 +566,28 @@
             dma((6, 7)), dma((6, 7)), dma((6, 8)), dma((6, 8)), dma((6, 3)),
         ],
         compiler_params=pltpu.CompilerParams(
-            collective_id=0, has_side_effects=True, vmem_limit_bytes=24 * 1024 * 1024),
-    )(gg, gd, *weights, *m, *v)
+            collective_id=0, has_side_effects=True, vmem_limit_bytes=16 * 1024 * 1024),
+    )(*(pltpu.with_memory_space_constraint(t, pltpu.HBM) for t in (gg, gd, *weights, *m, *v)))
+
+
+def out_kernel(n, *refs):
+    copies = [pltpu.make_async_copy(refs[i], refs[n + i], refs[2 * n].at[i]) for i in range(n)]
+    for c in copies:
+        c.start()
+    for c in copies:
+        c.wait()
+
+
+def put_out(arrays):
+    n = len(arrays)
+    return pl.pallas_call(
+        functools.partial(out_kernel, n),
+        out_shape=[jax.ShapeDtypeStruct(t.shape, t.dtype) for t in arrays],
+        in_specs=[pl.BlockSpec(memory_space=pl.ANY)] * n,
+        out_specs=[pl.BlockSpec(memory_space=pltpu.HBM)] * n,
+        scratch_shapes=[pltpu.SemaphoreType.DMA((n,))],
+        compiler_params=pltpu.CompilerParams(vmem_limit_bytes=1024 * 1024),
+    )(*arrays)
 
 
 def solution(mesh):
@@ -563,7 +596,7 @@
         gg, gd = grads(x[0], dy[0], *weights)
         blocks = [w.reshape(2, 16, -1, w.shape[-1]) for w in weights]
         count = float(sum(w.size for w in weights))
-        out = update(count, gg, gd, blocks, m, v)
+        out = put_out(update(count, gg, gd, blocks, m, v))
         return (*(o.reshape(w.shape) for o, w in zip(out[:3], weights)), *out[3:])
 
     whole, rows = P(None, None, None), P(None, "dp", None)

time: 395 us -> 347 us (0.88)
  local copies, waits for them, and re-layouts: 32.6 us -> 0 us
  Pallas kernels: 360 us -> 346 us
    unnamed x35 -> x0, local copies, waits for them, and re-layouts: 32.6 us -> none
    pallas_call x1, Pallas kernels: 255 us -> 232 us  [grads(): pl.pallas_call(grad_kernel, out_shape=[s((2, 2, 40, FF), BF16), s((2, 160...]
    pallas_call x0 -> x1, Pallas kernels: none -> 8.31 us  [put_out(): pl.pallas_call(functools.partial(out_kernel, n), out_shape=[jax.ShapeDtyp...]
where the time goes in v3:
time: 347 us
  Pallas kernels  346 us (100%)
    pallas_call x1, Pallas kernels, grads(): pl.pallas_call(grad_kernel, out_shape=[s((2, 2, 40, FF), BF16), s((2, 160...  232 us
    pallas_call x1, Pallas kernels, update(): pl.pallas_call(functools.partial(update_kernel, count), out_shape=[*(jax....  105 us
    pallas_call x1, Pallas kernels, put_out(): pl.pallas_call(functools.partial(out_kernel, n), out_shape=[jax.ShapeDtyp...  8.31 us

profile of v3, /device:TPU:0, one launch (start us, length us, event | category | flops | bytes accessed | tf_op | source)
XLA Modules:
  0.0 346.8 jit_solution(9029858900777306662)
XLA Ops:
  0.6 232.4 %shard_map.178 = (bf16[2,2,40,2560]{3,2,1,0:T(8,128)(2,1)}, bf16[2,160,640]{2,1,0:T(8,128)(2,1)}, f32[2,10,2048,256]{3,2,1,0:T(8,128)}, bf16[10,2048,256]{2,1,0:T(8,128)(2,1)}) custom-call(bf16[2048,640]{1,0:T(8,128)(2,1)} %bitcast.11, bf16[2048,640]{1,0:T(8,128)(2,1)} %bitcast.12, bf16[2,640,2560]{2,1,0:T(8,128)(2,1)} %wg_hbm.1, ...), custom_call_target="tpu_custom_call" | custom-call | tf_op jit(solution)/shard_map/pallas_call | solution.py:403
  233.0 105.3 %shard_map.179 = (bf16[2,16,40,2560]{3,2,1,0:T(8,128)(2,1)S(1)}, bf16[2,16,40,2560]{3,2,1,0:T(8,128)(2,1)S(1)}, bf16[2,16,160,640]{3,2,1,0:T(8,128)(2,1)S(1)}, f...) custom-call(bf16[2,2,40,2560]{3,2,1,0:T(8,128)(2,1)} %get-tuple-elem, ...), custom_call_target="tpu_custom_call" | custom-call | tf_op jit(solution)/shard_map/pallas_call | solution.py:554
  338.3 8.3 %shard_map.180 = (bf16[2,16,40,2560]{3,2,1,0:T(8,128)(2,1)}, bf16[2,16,40,2560]{3,2,1,0:T(8,128)(2,1)}, bf16[2,16,160,640]{3,2,1,0:T(8,128)(2,1)}, f32[2,40,2560...) custom-call(bf16[2,16,40,2560]{3,2,1,0:T(8,128)(2,1)S(1)} %get-tuple, ...), custom_call_target="tpu_custom_call" | custom-call | tf_op jit(solution)/shard_map/pallas_call | solution.py:583

commit v4 on v3

--- a/solution.py
+++ b/solution.py
@@ -15,8 +15,11 @@
 TILES = FF // F
 R = 512
 STEPS = T // R
+PIECE = 64
 DEPTH = 4
-HOPS = 7
+UP, DOWN = 4, 3
+HOPS = UP + DOWN
+ROUNDS = UP + 1
 L0 = TILES + 2
 LAST = L0 + TILES
 
@@ -114,33 +117,37 @@
     x_copy.wait()
     dy_copy.start()
 
-    def owner(s):
-        return ring((place - way * (1 + s) + 16) % 8)
+    def ahead(s):
+        return (place + way * (UP - s) + 16) % 8
+
+    def behind(s):
+        return (place - way * (DOWN - s) + 16) % 8
 
     def half(i):
         return remote(own.at[i % TILES, :, 1 - core], other.at[i], half_send.at[i], half_recv.at[i], rep, partner)
 
-    def hop_copy(i, s, src):
-        return remote(src, hop.at[i, s], hop_send.at[i, s], hop_recv.at[i, s], rep, to)
+    def hop_copy(i, slot, src):
+        return remote(src, hop.at[i, slot], hop_send.at[i, slot], hop_recv.at[i, slot], rep, to if slot < UP else back)
 
     def added(i, who):
         return own.at[i % TILES, who, core][...].astype(F32) + other.at[i, who][...].astype(F32)
 
-    def half_d(d, q):
-        rows_ = pl.ds(pl.multiple_of((2 * q + 1 - core) * 160, 32), 160)
-        return remote(ownd.at[d, rows_], otherd.at[d, q], dhalf_send.at[d, q], dhalf_recv.at[d, q], rep, partner)
-
-    def hop_copy_d(d, s, src):
-        return remote(src, hopd.at[d, s], dhop_send.at[d, s], dhop_recv.at[d, s], rep, to)
+    def half_d(d, who):
+        rows_ = pl.ds(pl.multiple_of((2 * who + 1 - core) * 160, 32), 160)
+        return remote(ownd.at[d, rows_], otherd.at[d, who], dhalf_send.at[d, who], dhalf_recv.at[d, who], rep, partner)
+
+    def hop_copy_d(d, slot, src, device):
+        return remote(src, hopd.at[d, slot], dhop_send.at[d, slot], dhop_recv.at[d, slot], rep, device)
 
     def rows_d(who):
         return pl.ds(pl.multiple_of((2 * who + core) * 160, 32), 160)
 
     def added_d(d, who):
+        half_d(d, who).wait_recv()
         return ownd.at[d, rows_d(who)][...].astype(F32) + otherd.at[d, who][...].astype(F32)
 
     def serve(n):
-        for age in range(1, HOPS + 2):
+        for age in range(1, ROUNDS + 1):
             c = n - age
             late = jnp.where(c >= L0, 1, 0)
             i = c - 2 * late
@@ -150,57 +157,68 @@
                 s = age - 1
                 if s == 0:
                     half(i).wait_recv()
-                    mine = own.at[i % TILES, owner(0), core]
-                    mine[...] = added(i, owner(0)).astype(BF16)
-                    hop_copy(i, 0, mine).start()
+                    for slot, p in ((0, ahead(0)), (UP, behind(0))):
+                        mine = own.at[i % TILES, ring(p), core]
+                        mine[...] = added(i, ring(p)).astype(BF16)
+                        hop_copy(i, slot, mine).start()
+                elif s < UP:
+                    for slot, p in ((s, ahead(s)), (UP + s, behind(s)))[: 2 if s < DOWN else 1]:
+                        before = hop.at[i, slot - 1]
+                        hop_copy(i, slot - 1, before).wait_recv()
+                        before[...] = (before[...].astype(F32) + added(i, ring(p))).astype(BF16)
+                        hop_copy(i, slot, before).start()
                 else:
-                    slot = hop.at[i, s - 1]
-                    hop_copy(i, s - 1, slot).wait_recv()
-                    who = owner(s)
-                    new = (slot[...].astype(F32) + added(i, who)).astype(BF16)
-                    if s < HOPS:
-                        slot[...] = new
-                        hop_copy(i, s, slot).start()
-                    else:
-                        gg.at[1 - late][:, :, cols(i % TILES)] = new
-                        half(i).wait_send()
-                        for r in range(HOPS):
-                            hop_copy(i, r, slot).wait_send()
-
-    def serve_d(d, age):
+                    one, two = hop.at[i, UP - 1], hop.at[i, HOPS - 1]
+                    hop_copy(i, UP - 1, one).wait_recv()
+                    hop_copy(i, HOPS - 1, two).wait_recv()
+                    new = (one[...].astype(F32) + two[...].astype(F32) + added(i, chip)).astype(BF16)
+                    gg.at[1 - late][:, :, cols(i % TILES)] = new
+                    half(i).wait_send()
+                    for r in range(HOPS):
+                        hop_copy(i, r, one).wait_send()
+
+    def quarter(p):
+        t = p // 2
+        return t + (t // 2) * (5 - 2 * t)
+
+    def ready(q):
+        return (5 * (q + 1) - 1) // 2
+
+    def serve_d(d, q, age):
         s = age - 1
-
-        @pl.when(s == 0)
+        for base, hops, place_of, device in ((0, UP, ahead, to), (UP, DOWN, behind, back)):
+            p = place_of(s)
+            here = quarter(p) == q
+
+            @pl.when((s == 0) & here)
+            def _():
+                mine = ownd.at[d, rows_d(ring(p))]
+                mine[...] = added_d(d, ring(p)).astype(BF16)
+                hop_copy_d(d, base, mine, device).start()
+
+            @pl.when((s > 0) & (s < hops) & here)
+            def _():
+                before = hopd.at[d, base + s - 1]
+                hop_copy_d(d, base + s - 1, before, device).wait_recv()
+                before[...] = (before[...].astype(F32) + added_d(d, ring(p))).astype(BF16)
+                hop_copy_d(d, base + s, before, device).start()
+
+        @pl.when((s == UP) & (quarter(place) == q))
         def _():
-            for q in range(8):
-                half_d(d, q).wait_recv()
-            mine = ownd.at[d, rows_d(owner(0))]
-            mine[...] = added_d(d, owner(0)).astype(BF16)
-            hop_copy_d(d, 0, mine).start()
-
-        @pl.when((s > 0) & (s <= HOPS))
-        def _():
-            slot = hopd.at[d, s - 1]
-            hop_copy_d(d, s - 1, slot).wait_recv()
-            new = (slot[...].astype(F32) + added_d(d, owner(s))).astype(BF16)
-
-            @pl.when(s < HOPS)
-            def _():
-                slot[...] = new
-                hop_copy_d(d, s, slot).start()
-
-            @pl.when(s == HOPS)
-            def _():
-                gd.at[d][...] = new
-                for q in range(8):
-                    half_d(d, q).wait_send()
-                for r in range(HOPS):
-                    hop_copy_d(d, r, slot).wait_send()
+            one, two = hopd.at[d, UP - 1], hopd.at[d, HOPS - 1]
+            hop_copy_d(d, UP - 1, one, to).wait_recv()
+            hop_copy_d(d, HOPS - 1, two, back).wait_recv()
+            gd.at[d][...] = (one[...].astype(F32) + two[...].astype(F32) + added_d(d, chip)).astype(BF16)
 
     def put(i, n, t_, grad):
         g = dot(t_[...], grad[...]).astype(BF16)
         for o in range(16):
             own.at[i % TILES, o // 2, o % 2, n][...] = g[40 * o : 40 * o + 40]
+
+    def pieces(t):
+        for i in range(0, R, PIECE):
+            at = t * R + i
+            yield slice(i, i + PIECE), pl.ds(at if isinstance(t, int) else pl.multiple_of(at, PIECE), PIECE)
 
     def norm(t, to_t):
         wide = h[rows(t), :].astype(F32)
@@ -230,16 +248,17 @@
             h_slot, w_slot, t_before = before
             acc[rows(t_before), :] += dot(hid[h_slot, rows(t_before), :], wd[w_slot])
             gate, up = dot(a[rows(t), :], wg[j % 2]), dot(a[rows(t), :], wu[j % 2])
-            hidden = (gate * sigmoid(gate) * up).astype(BF16)
 
             @pl.when(k >= DEPTH)
             def _():
                 for c in gu_copies(k - DEPTH, True):
                     c.wait()
 
-            gu.at[k % DEPTH, 0][...] = gate
-            gu.at[k % DEPTH, 1][...] = up
-            hid.at[j % 3][rows(t), :] = hidden
+            for here, there in pieces(t):
+                one, two = gate[here], up[here]
+                gu.at[k % DEPTH, 0][here, :] = one
+                gu.at[k % DEPTH, 1][here, :] = two
+                hid.at[j % 3][there, :] = (one * sigmoid(one) * two).astype(BF16)
             for c in gu_copies(k, True):
                 c.start()
 
@@ -267,12 +286,13 @@
     dy_copy.wait()
     pl.semaphore_wait(barrier, 3)
 
-    def back_of(gate, up, by_hidden, slot, t):
+    def back_of(gate, up, by_hidden, there, to_hidden=None):
         sig = sigmoid(gate)
         silu = gate * sig
-        dg[rows(t), :] = (by_hidden * up * (sig + silu * (1.0 - sig))).astype(BF16)
-        du[rows(t), :] = (by_hidden * silu).astype(BF16)
-        return silu
+        dg[there, :] = (by_hidden * up * (sig + silu * (1.0 - sig))).astype(BF16)
+        du[there, :] = (by_hidden * silu).astype(BF16)
+        if to_hidden is not None:
+            to_hidden[there, :] = (silu * up).astype(BF16)
 
     def tile(j, z):
         k = TILES + j
@@ -283,17 +303,30 @@
         def step(t, z):
             gate, up = dot(a[rows(t), :], wg[slot]), dot(a[rows(t), :], wu[slot])
             by_hidden = dot_nt(dy[rows(t), :], wd[slot]).astype(BF16).astype(F32)
-            silu = back_of(gate, up, by_hidden, slot, t)
-            hid.at[0][rows(t), :] = (silu * up).astype(BF16)
+            for here, there in pieces(t):
+                back_of(gate[here], up[here], by_hidden[here], there, hid.at[0])
             return z
 
         for t in range(STEPS):
             step(t, 0)
         serve(j)
+
+        def quarters(q, z):
+            serve_d(1, q, j - ready(q))
+            return z
+
+        lax.fori_loop(0, 3, quarters, 0)
         put(j, 0, a1t, dg)
         put(j, 1, a1t, du)
         half(j).start()
         ownd.at[1][cols(j), :] = dot_tn(hid[0], dy[...]).astype(BF16)
+
+        for q in range(4):
+            @pl.when(j == ready(q))
+            def _():
+                half_d(1, 2 * q).start()
+                half_d(1, 2 * q + 1).start()
+
 
         def step_a(t, z):
             acc[rows(t), :] += dot_nt(dg[rows(t), :], wg[slot]) + dot_nt(du[rows(t), :], wu[slot])
@@ -310,8 +343,6 @@
         return z
 
     lax.fori_loop(0, TILES, tile, 0)
-    for q in range(8):
-        half_d(1, q).start()
     hid_copy(0, False).start()
     hid_copy(1, False).start()
     for k in range(DEPTH - 1):
@@ -341,26 +372,45 @@
             return z
 
         lax.fori_loop(0, TILES // 2, one, 0)
+        for i in range(4):
+            half_d(0, 4 * r + i).start()
         serve(TILES + r)
-        serve_d(1, 1 + r)
+
+        def quarters(q, z):
+            serve_d(1, q, TILES + r - ready(q))
+            serve_d(0, q, r - q // 2)
+            return z
+
+        lax.fori_loop(0, 4, quarters, 0)
         return z
 
     lax.fori_loop(0, 2, down, 0)
-    for q in range(8):
-        half_d(0, q).start()
+
+    def wd_copy(k):
+        return pltpu.make_async_copy(wd_hbm.at[0, cols(k % TILES), :], wd.at[k % 2], w_sem.at[2, k % 2])
+
+    w_wait(2 * TILES)
+    wd_copy(2 * TILES + 1).start()
+
+    def by_hidden(t, z):
+        hid.at[0][rows(t), :] = dot_nt(dy[rows(t), :], wd[0]).astype(BF16)
+        return z
+
+    lax.fori_loop(0, STEPS, by_hidden, 0)
 
     def tile0(j, z):
         k = 2 * TILES + j
-        slot = k % 2
-        w_wait(k)
 
         @pl.when(j + 1 < TILES)
         def _():
-            w_start(k + 1)
+            wd_copy(k + 1).wait()
+
+        @pl.when(j + 2 < TILES)
+        def _():
+            wd_copy(k + 2).start()
 
         def step(t, z):
             n = j * STEPS + t
-            by_hidden = dot_nt(dy[rows(t), :], wd[slot]).astype(BF16).astype(F32)
             for c in gu_copies(n, False):
                 c.wait()
 
@@ -369,13 +419,20 @@
                 for c in gu_copies(n + DEPTH - 1, False):
                     c.start()
 
-            back_of(gu[n % DEPTH, 0], gu[n % DEPTH, 1], by_hidden, slot, t)
+            hid.at[(j + 1) % 2][rows(t), :] = dot_nt(dy[rows(t), :], wd[(j + 1) % 2]).astype(BF16)
+            for here, there in pieces(t):
+                back_of(gu[n % DEPTH, 0, here, :], gu[n % DEPTH, 1, here, :], hid[j % 2, there, :].astype(F32), there)
             return z
 
         lax.fori_loop(0, STEPS, step, 0)
         serve(L0 + j)
-        serve_d(1, 3 + j)
-        serve_d(0, 1 + j)
+
+        def quarters(q, z):
+            serve_d(1, q, L0 + j - ready(q))
+            serve_d(0, q, 2 + j - q // 2)
+            return z
+
+        lax.fori_loop(0, 4, quarters, 0)
         put(TILES + j, 0, a0t, dg)
         put(TILES + j, 1, a0t, du)
         half(TILES + j).start()
@@ -387,7 +444,12 @@
         serve(LAST + r)
         return z
 
-    lax.fori_loop(0, HOPS + 1, drain, 0)
+    lax.fori_loop(0, ROUNDS, drain, 0)
+    for d in range(2):
+        for who in range(8):
+            half_d(d, who).wait_send()
+        for slot in range(HOPS):
+            hop_copy_d(d, slot, hopd.at[d, slot], to).wait_send()
     out = [pltpu.make_async_copy(gg, gg_hbm, io_sem.at[0]), pltpu.make_async_copy(gd, gd_hbm, io_sem.at[1])]
     for c in out:
         c.start()

time: 347 us -> 348 us (level)
  no operation moved by 1% of the time
where the time goes in v4:
time: 348 us
  Pallas kernels  347 us (100%)
    pallas_call x1, Pallas kernels, grads(): pl.pallas_call(grad_kernel, out_shape=[s((2, 2, 40, FF), BF16), s((2, 160...  233 us
    pallas_call x1, Pallas kernels, update(): pl.pallas_call(functools.partial(update_kernel, count), out_shape=[*(jax....  106 us
    pallas_call x1, Pallas kernels, put_out(): pl.pallas_call(functools.partial(out_kernel, n), out_shape=[jax.ShapeDtyp...  8.31 us

profile of v4, /device:TPU:0, one launch (start us, length us, event | category | flops | bytes accessed | tf_op | source)
XLA Modules:
  0.0 348.1 jit_solution(1333035505721324862)
XLA Ops:
  0.6 232.6 %shard_map.178 = (bf16[2,2,40,2560]{3,2,1,0:T(8,128)(2,1)}, bf16[2,160,640]{2,1,0:T(8,128)(2,1)}, f32[2,10,2048,256]{3,2,1,0:T(8,128)}, bf16[10,2048,256]{2,1,0:T(8,128)(2,1)}) custom-call(bf16[2048,640]{1,0:T(8,128)(2,1)} %bitcast.11, bf16[2048,640]{1,0:T(8,128)(2,1)} %bitcast.12, bf16[2,640,2560]{2,1,0:T(8,128)(2,1)} %wg_hbm.1, ...), custom_call_target="tpu_custom_call" | custom-call | tf_op jit(solution)/shard_map/pallas_call | solution.py:465
  233.2 106.3 %shard_map.179 = (bf16[2,16,40,2560]{3,2,1,0:T(8,128)(2,1)S(1)}, bf16[2,16,40,2560]{3,2,1,0:T(8,128)(2,1)S(1)}, bf16[2,16,160,640]{3,2,1,0:T(8,128)(2,1)S(1)}, f...) custom-call(bf16[2,2,40,2560]{3,2,1,0:T(8,128)(2,1)} %get-tuple-elem, ...), custom_call_target="tpu_custom_call" | custom-call | tf_op jit(solution)/shard_map/pallas_call | solution.py:616
  339.6 8.3 %shard_map.180 = (bf16[2,16,40,2560]{3,2,1,0:T(8,128)(2,1)}, bf16[2,16,40,2560]{3,2,1,0:T(8,128)(2,1)}, bf16[2,16,160,640]{3,2,1,0:T(8,128)(2,1)}, f32[2,40,2560...) custom-call(bf16[2,16,40,2560]{3,2,1,0:T(8,128)(2,1)S(1)} %get-tuple, ...), custom_call_target="tpu_custom_call" | custom-call | tf_op jit(solution)/shard_map/pallas_call | solution.py:645

commit v5 on v4

--- a/solution.py
+++ b/solution.py
@@ -62,7 +62,7 @@
 
 def grad_kernel(x_hbm, dy_hbm, wg_hbm, wu_hbm, wd_hbm,
                 gg_hbm, gd_hbm, gu_hbm, hid_hbm,
-                h, a, a0t, a1t, dy, acc, hid, dg, du, wg, wu, wd, gu,
+                h, a, a0t, a1t, dy, acc, hid, dg, du, wg, wu, wd, wgt, wut, wdt, gu,
                 own, other, hop, ownd, otherd, hopd, gg, gd,
                 io_sem, w_sem, gu_sem, hid_sem,
                 half_send, half_recv, hop_send, hop_recv, dhalf_send, dhalf_recv, dhop_send, dhop_recv):
@@ -302,11 +302,12 @@
 
         def step(t, z):
             gate, up = dot(a[rows(t), :], wg[slot]), dot(a[rows(t), :], wu[slot])
-            by_hidden = dot_nt(dy[rows(t), :], wd[slot]).astype(BF16).astype(F32)
+            by_hidden = dot(dy[rows(t), :], wdt[...]).astype(BF16).astype(F32)
             for here, there in pieces(t):
                 back_of(gate[here], up[here], by_hidden[here], there, hid.at[0])
             return z
 
+        wdt[...] = wd[slot].T
         for t in range(STEPS):
             step(t, 0)
         serve(j)
@@ -316,6 +317,8 @@
             return z
 
         lax.fori_loop(0, 3, quarters, 0)
+        wgt[...] = wg[slot].T
+        wut[...] = wu[slot].T
         put(j, 0, a1t, dg)
         put(j, 1, a1t, du)
         half(j).start()
@@ -329,7 +332,7 @@
 
 
         def step_a(t, z):
-            acc[rows(t), :] += dot_nt(dg[rows(t), :], wg[slot]) + dot_nt(du[rows(t), :], wu[slot])
+            acc[rows(t), :] += dot(dg[rows(t), :], wgt[...]) + dot(du[rows(t), :], wut[...])
             return z
 
         @pl.when(j == 0)
@@ -378,7 +381,7 @@
 
         def quarters(q, z):
             serve_d(1, q, TILES + r - ready(q))
-            serve_d(0, q, r - q // 2)
+            serve_d(0, q, r - 2 * q)
             return z
 
         lax.fori_loop(0, 4, quarters, 0)
@@ -429,7 +432,7 @@
 
         def quarters(q, z):
             serve_d(1, q, L0 + j - ready(q))
-            serve_d(0, q, 2 + j - q // 2)
+            serve_d(0, q, 2 + j - 2 * q)
             return z
 
         lax.fori_loop(0, 4, quarters, 0)
@@ -471,7 +474,8 @@
         scratch_shapes=[
             vmem((T, D), BF16), vmem((T, D), BF16), vmem((D, T), BF16), vmem((D, T), BF16), vmem((T, D), BF16),
             vmem((T, D), F32), vmem((3, T, F), BF16), vmem((T, F), BF16), vmem((T, F), BF16),
-            vmem((2, D, F), BF16), vmem((2, D, F), BF16), vmem((2, F, D), BF16), vmem((DEPTH, 2, R, F), F32),
+            vmem((2, D, F), BF16), vmem((2, D, F), BF16), vmem((2, F, D), BF16),
+            vmem((F, D), BF16), vmem((F, D), BF16), vmem((D, F), BF16), vmem((DEPTH, 2, R, F), F32),
             vmem((TILES, 8, 2, *block), BF16), vmem((2 * TILES, 8, *block), BF16), vmem((2 * TILES, HOPS, *block), BF16),
             vmem((2, FF, D), BF16), vmem((2, 8, 160, D), BF16), vmem((2, HOPS, 160, D), BF16),
             vmem((2, 2, 40, FF), BF16), vmem((2, 160, D), BF16),

time: 348 us -> 361 us (1.037)
  Pallas kernels: 347 us -> 360 us
    pallas_call x1, Pallas kernels: 233 us -> 245 us  [grads(): pl.pallas_call(grad_kernel, out_shape=[s((2, 2, 40, FF), BF16), s((2, 160...]
where the time goes in v5:
time: 361 us
  Pallas kernels  360 us (100%)
    pallas_call x1, Pallas kernels, grads(): pl.pallas_call(grad_kernel, out_shape=[s((2, 2, 40, FF), BF16), s((2, 160...  245 us
    pallas_call x1, Pallas kernels, update(): pl.pallas_call(functools.partial(update_kernel, count), out_shape=[*(jax....  107 us
    pallas_call x1, Pallas kernels, put_out(): pl.pallas_call(functools.partial(out_kernel, n), out_shape=[jax.ShapeDtyp...  8.31 us

profile of v5, /device:TPU:0, one launch (start us, length us, event | category | flops | bytes accessed | tf_op | source)
XLA Modules:
  0.0 360.8 jit_solution(12716979843083257639)
XLA Ops:
  0.6 244.6 %shard_map.178 = (bf16[2,2,40,2560]{3,2,1,0:T(8,128)(2,1)}, bf16[2,160,640]{2,1,0:T(8,128)(2,1)}, f32[2,10,2048,256]{3,2,1,0:T(8,128)}, bf16[10,2048,256]{2,1,0:T(8,128)(2,1)}) custom-call(bf16[2048,640]{1,0:T(8,128)(2,1)} %bitcast.11, bf16[2048,640]{1,0:T(8,128)(2,1)} %bitcast.12, bf16[2,640,2560]{2,1,0:T(8,128)(2,1)} %wg_hbm.1, ...), custom_call_target="tpu_custom_call" | custom-call | tf_op jit(solution)/shard_map/pallas_call | solution.py:468
  245.3 107.1 %shard_map.179 = (bf16[2,16,40,2560]{3,2,1,0:T(8,128)(2,1)S(1)}, bf16[2,16,40,2560]{3,2,1,0:T(8,128)(2,1)S(1)}, bf16[2,16,160,640]{3,2,1,0:T(8,128)(2,1)S(1)}, f...) custom-call(bf16[2,2,40,2560]{3,2,1,0:T(8,128)(2,1)} %get-tuple-elem, ...), custom_call_target="tpu_custom_call" | custom-call | tf_op jit(solution)/shard_map/pallas_call | solution.py:620
  352.4 8.3 %shard_map.180 = (bf16[2,16,40,2560]{3,2,1,0:T(8,128)(2,1)}, bf16[2,16,40,2560]{3,2,1,0:T(8,128)(2,1)}, bf16[2,16,160,640]{3,2,1,0:T(8,128)(2,1)}, f32[2,40,2560...) custom-call(bf16[2,16,40,2560]{3,2,1,0:T(8,128)(2,1)S(1)} %get-tuple, ...), custom_call_target="tpu_custom_call" | custom-call | tf_op jit(solution)/shard_map/pallas_call | solution.py:649

commit v6 on v5

--- a/solution.py
+++ b/solution.py
@@ -381,7 +381,6 @@
 
         def quarters(q, z):
             serve_d(1, q, TILES + r - ready(q))
-            serve_d(0, q, r - 2 * q)
             return z
 
         lax.fori_loop(0, 4, quarters, 0)
@@ -432,7 +431,7 @@
 
         def quarters(q, z):
             serve_d(1, q, L0 + j - ready(q))
-            serve_d(0, q, 2 + j - 2 * q)
+            serve_d(0, q, jnp.where(j % 2 == 0, j // 2 + 1, 0))
             return z
 
         lax.fori_loop(0, 4, quarters, 0)

time: 361 us -> 346 us (0.958)
  Pallas kernels: 360 us -> 345 us
    pallas_call x1, Pallas kernels: 245 us -> 232 us  [grads(): pl.pallas_call(grad_kernel, out_shape=[s((2, 2, 40, FF), BF16), s((2, 160...]
where the time goes in v6:
time: 346 us
  Pallas kernels  345 us (100%)
    pallas_call x1, Pallas kernels, grads(): pl.pallas_call(grad_kernel, out_shape=[s((2, 2, 40, FF), BF16), s((2, 160...  232 us
    pallas_call x1, Pallas kernels, update(): pl.pallas_call(functools.partial(update_kernel, count), out_shape=[*(jax....  105 us
    pallas_call x1, Pallas kernels, put_out(): pl.pallas_call(functools.partial(out_kernel, n), out_shape=[jax.ShapeDtyp...  8.31 us

profile of v6, /device:TPU:0, one launch (start us, length us, event | category | flops | bytes accessed | tf_op | source)
XLA Modules:
  0.0 345.9 jit_solution(8854112294808176696)
XLA Ops:
  0.6 231.6 %shard_map.178 = (bf16[2,2,40,2560]{3,2,1,0:T(8,128)(2,1)}, bf16[2,160,640]{2,1,0:T(8,128)(2,1)}, f32[2,10,2048,256]{3,2,1,0:T(8,128)}, bf16[10,2048,256]{2,1,0:T(8,128)(2,1)}) custom-call(bf16[2048,640]{1,0:T(8,128)(2,1)} %bitcast.11, bf16[2048,640]{1,0:T(8,128)(2,1)} %bitcast.12, bf16[2,640,2560]{2,1,0:T(8,128)(2,1)} %wg_hbm.1, ...), custom_call_target="tpu_custom_call" | custom-call | tf_op jit(solution)/shard_map/pallas_call | solution.py:467
  232.3 105.1 %shard_map.179 = (bf16[2,16,40,2560]{3,2,1,0:T(8,128)(2,1)S(1)}, bf16[2,16,40,2560]{3,2,1,0:T(8,128)(2,1)S(1)}, bf16[2,16,160,640]{3,2,1,0:T(8,128)(2,1)S(1)}, f...) custom-call(bf16[2,2,40,2560]{3,2,1,0:T(8,128)(2,1)} %get-tuple-elem, ...), custom_call_target="tpu_custom_call" | custom-call | tf_op jit(solution)/shard_map/pallas_call | solution.py:619
  337.4 8.3 %shard_map.180 = (bf16[2,16,40,2560]{3,2,1,0:T(8,128)(2,1)}, bf16[2,16,40,2560]{3,2,1,0:T(8,128)(2,1)}, bf16[2,16,160,640]{3,2,1,0:T(8,128)(2,1)}, f32[2,40,2560...) custom-call(bf16[2,16,40,2560]{3,2,1,0:T(8,128)(2,1)S(1)} %get-tuple, ...), custom_call_target="tpu_custom_call" | custom-call | tf_op jit(solution)/shard_map/pallas_call | solution.py:648

commit v7 on v6

--- a/solution.py
+++ b/solution.py
@@ -429,12 +429,19 @@
         lax.fori_loop(0, STEPS, step, 0)
         serve(L0 + j)
 
-        def quarters(q, z):
-            serve_d(1, q, L0 + j - ready(q))
-            serve_d(0, q, jnp.where(j % 2 == 0, j // 2 + 1, 0))
-            return z
-
-        lax.fori_loop(0, 4, quarters, 0)
+        @pl.when(j < 3)
+        def _():
+            for q in (2, 3):
+                serve_d(1, q, L0 + j - ready(q))
+
+        @pl.when(j % 2 == 0)
+        def _():
+            def quarters(q, z):
+                serve_d(0, q, j // 2 + 1)
+                return z
+
+            lax.fori_loop(0, 4, quarters, 0)
+
         put(TILES + j, 0, a0t, dg)
         put(TILES + j, 1, a0t, du)
         half(TILES + j).start()

time: 346 us -> 344 us (level)
  no operation moved by 1% of the time
where the time goes in v7:
time: 344 us; the launch traced here: 343 us
  Pallas kernels  343 us (100%)
    pallas_call x1, Pallas kernels, grads(): pl.pallas_call(grad_kernel, out_shape=[s((2, 2, 40, FF), BF16), s((2, 160...  229 us
    pallas_call x1, Pallas kernels, update(): pl.pallas_call(functools.partial(update_kernel, count), out_shape=[*(jax....  105 us
    pallas_call x1, Pallas kernels, put_out(): pl.pallas_call(functools.partial(out_kernel, n), out_shape=[jax.ShapeDtyp...  8.31 us

profile of v7, /device:TPU:0, one launch (start us, length us, event | category | flops | bytes accessed | tf_op | source)
XLA Modules:
  0.0 343.5 jit_solution(17213119227633214948)
XLA Ops:
  0.6 229.3 %shard_map.178 = (bf16[2,2,40,2560]{3,2,1,0:T(8,128)(2,1)}, bf16[2,160,640]{2,1,0:T(8,128)(2,1)}, f32[2,10,2048,256]{3,2,1,0:T(8,128)}, bf16[10,2048,256]{2,1,0:T(8,128)(2,1)}) custom-call(bf16[2048,640]{1,0:T(8,128)(2,1)} %bitcast.11, bf16[2048,640]{1,0:T(8,128)(2,1)} %bitcast.12, bf16[2,640,2560]{2,1,0:T(8,128)(2,1)} %wg_hbm.1, ...), custom_call_target="tpu_custom_call" | custom-call | tf_op jit(solution)/shard_map/pallas_call | solution.py:474
  230.0 105.0 %shard_map.179 = (bf16[2,16,40,2560]{3,2,1,0:T(8,128)(2,1)S(1)}, bf16[2,16,40,2560]{3,2,1,0:T(8,128)(2,1)S(1)}, bf16[2,16,160,640]{3,2,1,0:T(8,128)(2,1)S(1)}, f...) custom-call(bf16[2,2,40,2560]{3,2,1,0:T(8,128)(2,1)} %get-tuple-elem, ...), custom_call_target="tpu_custom_call" | custom-call | tf_op jit(solution)/shard_map/pallas_call | solution.py:626
  335.0 8.3 %shard_map.180 = (bf16[2,16,40,2560]{3,2,1,0:T(8,128)(2,1)}, bf16[2,16,40,2560]{3,2,1,0:T(8,128)(2,1)}, bf16[2,16,160,640]{3,2,1,0:T(8,128)(2,1)}, f32[2,40,2560...) custom-call(bf16[2,16,40,2560]{3,2,1,0:T(8,128)(2,1)S(1)} %get-tuple, ...), custom_call_target="tpu_custom_call" | custom-call | tf_op jit(solution)/shard_map/pallas_call | solution.py:655
